TPU v7x, 8 devices: a whole 2x2x1 slice. The times are simulated.
8 devices in a mesh: dp: 1 (over z), cp: 8 (over y, x, core).
Axes of the slice: x: 2, y: 2, z: 1, core: 2. Of those that a mesh axis runs over, the one named last changes fastest.
Arguments:
- q_tok: bfloat16 [8192, 2, 128], P(('dp', 'cp'))
- k_tok: bfloat16 [8192, 128], P(('dp', 'cp'))
- v_tok: bfloat16 [8192, 128], P(('dp', 'cp'))
- fwd_out: bfloat16 [8192, 2, 128], P(('dp', 'cp'))
- d_out: bfloat16 [8192, 2, 128], P(('dp', 'cp'))
- lse_row: float32 [8192, 2], P(('dp', 'cp'))
Outputs:
- output 1: bfloat16 [8192, 2, 128], P(('dp', 'cp'))
- output 2: bfloat16 [8192, 128], P(('dp', 'cp'))
- output 3: bfloat16 [8192, 128], P(('dp', 'cp'))
All inputs are finite; a program needn't handle non-finite values.
Results may differ from a plain program's by a relative error of at most 0.001.
Values are sent between devices in bfloat16 or wider.
A program may use at most 1 GiB of HBM per device.

v0:
```python
import jax
import jax.numpy as jnp
from jax import lax
from jax.sharding import PartitionSpec as P


def pair_scores(q_block, do_block, lse_block, delta_block, k_block, v_block, on_diag, softmax_scale):
    logits = jnp.einsum('rgd,cd->rgc', q_block, k_block, preferred_element_type=jnp.float32)
    row_ids = jnp.arange(q_block.shape[0])
    allowed = jnp.logical_or(row_ids[None, :] <= row_ids[:, None], jnp.logical_not(on_diag))
    prob_mat = jnp.exp(jnp.where(allowed[:, None, :], logits * softmax_scale - lse_block[:, :, None], -jnp.inf))
    d_prob = jnp.einsum('rgd,cd->rgc', do_block, v_block, preferred_element_type=jnp.float32)
    d_score = (prob_mat * (d_prob - delta_block[:, :, None])).astype(jnp.bfloat16)
    return prob_mat.astype(jnp.bfloat16), d_score


def solution(mesh):
    n_dev = mesh.shape['cp']
    forward_perm = [(i, (i + 1) % n_dev) for i in range(n_dev)]
    row_spec = P(('dp', 'cp'))

    def local_fn(q_tok, k_tok, v_tok, fwd_out, d_out, lse_row):
        softmax_scale = q_tok.shape[-1] ** -0.5
        my_index = lax.axis_index('cp')
        row_delta = jnp.einsum('rgd,rgd->rg', d_out, fwd_out, preferred_element_type=jnp.float32)

        def accumulate(step, state):
            def pair_update(state_in):
                dq_acc, k_cur, v_cur, dk_acc, dv_acc = state_in
                prob_low, score_low = pair_scores(q_tok, d_out, lse_row, row_delta, k_cur, v_cur, step == 0, softmax_scale)
                dq_acc = dq_acc + jnp.einsum('rgc,cd->rgd', score_low, k_cur, preferred_element_type=jnp.float32)
                dk_acc = dk_acc + jnp.einsum('rgc,rgd->cd', score_low, q_tok, preferred_element_type=jnp.float32)
                dv_acc = dv_acc + jnp.einsum('rgc,rgd->cd', prob_low, d_out, preferred_element_type=jnp.float32)
                return (dq_acc, k_cur, v_cur, dk_acc, dv_acc)

            def keep_state(state_in):
                return state_in

            return lax.cond(step <= my_index, pair_update, keep_state, state)

        def step_fn(step, state):
            dq_acc, k_cur, v_cur, dk_acc, dv_acc = accumulate(step, state)
            k_next = lax.ppermute(k_cur, 'cp', forward_perm)
            v_next = lax.ppermute(v_cur, 'cp', forward_perm)
            dk_next = lax.ppermute(dk_acc, 'cp', forward_perm)
            dv_next = lax.ppermute(dv_acc, 'cp', forward_perm)
            return (dq_acc, k_next, v_next, dk_next, dv_next)

        kv_zeros = jnp.zeros(k_tok.shape, jnp.float32)
        state = (jnp.zeros(q_tok.shape, jnp.float32), k_tok, v_tok, kv_zeros, kv_zeros)
        state = lax.fori_loop(0, n_dev - 1, step_fn, state)
        dq_acc, k_cur, v_cur, dk_acc, dv_acc = accumulate(n_dev - 1, state)
        dk_home = lax.ppermute(dk_acc, 'cp', forward_perm)
        dv_home = lax.ppermute(dv_acc, 'cp', forward_perm)
        grad_q = (dq_acc * softmax_scale).astype(jnp.bfloat16)
        grad_k = (dk_home * softmax_scale).astype(jnp.bfloat16)
        grad_v = dv_home.astype(jnp.bfloat16)
        return grad_q, grad_k, grad_v

    return jax.shard_map(local_fn, mesh=mesh, in_specs=(row_spec, row_spec, row_spec, row_spec, row_spec, row_spec), out_specs=(row_spec, row_spec, row_spec), check_vma=False)
```

profile of v0, /device:TPU:0, one launch (start us, length us, event | category | flops | bytes accessed | tf_op | source)
XLA Modules:
  0.0 258.4 jit_solution(7556433833159893096)
XLA Ops:
  2.5 1.9 copy.14
  4.4 2.4 fusion.37
  7.0 1.1 copy.13
  9.1 224.9 %while.21 = (s32[]{:T(128)}, f32[1024,2,128]{2,0,1:T(8,128)S(1)}, bf16[1024,128]{1,0:T(8,128)(2,1)S(1)}, bf16[1024,128]{1,0:T(8,128)(2,1)S(1)}, f32[1024,128]{1,...) while((s32[]{:T(128)}, f32[1024,2,128]{2,0,1:T(8,128)S(1)}, ...), condition=%wide.region_3.4_spmd, body=%wide.region_0.3_spmd.sunk | while | flops 2707947520 | bytes 57467344 | solution.py:51
  9.8 13.4 %conditional.4 = ((f32[1024,2,128]{2,0,1:T(8,128)S(1)}, f32[1024,128]{1,0:T(8,128)S(1)}, f32[1024,128]{1,0:T(8,128)})) conditional(s32[]{:T(128)} %convert_element_type.52, (f32[1024,2,128]{2,0,1:T(8,128)S(1)}, f32[1024,128]{1,0:T(8,128)S(1)}, f32[1024,128]{1,0:T(8,128)}) %tuple.54, (s32[]{:T(128)}, bf16[1024,2,128]{2,0,1:T(8,128)(2,1)S(1)}, ...), branch_computations={%region_1.0_spmd, %region_2.2_spmd} | conditional | flops 2707947520 | bytes 48029768 | solution.py:39
  10.2 1.3 fusion.14
  11.5 4.9 %fusion.8 = f32[1024,128]{1,0:T(8,128)} fusion(f32[1024,128]{1,0:T(8,128)} %get-tuple-element.232, bf16[1024,2,128]{2,0,1:T(8,128)(2,1)} %get-tuple-element.228, f32[1024,2,1024]{2,0,1:T(8,128)S(1)} %fusion.14, f32[1024,2]{0,1:T(2,128)S(1)} %copy-done.2, pred[1024,1024]{1,0:T(8,128)(4,1)S(1)} %fusion.3), kind=kOutput, calls=%fused_computation.10 | convolution fusion | flops 545390592 | bytes 11018240 | tf_op jit(solution)/shard_map/while/body/eval_jaxpr/cond/branch_1_fun/rgc,rgd->cd/dot_general | solution.py:33
  16.3 4.2 %multiply_convert_fusion = bf16[1024,2,1024]{2,0,1:T(8,128)(2,1)S(1)} fusion(f32[1024,2,1024]{2,0,1:T(8,128)S(1)} %fusion.14, f32[1024,2]{0,1:T(2,128)S(1)} %get-tuple-element.230, f32[1024,2]{0,1:T(2,128)S(1)} %copy-done.2, pred[1024,1024]{1,0:T(8,128)(4,1)S(1)} %fusion.3, bf16[1024,2,128]{2,0,1:T(8,128)(2,1)} %get-tuple-element.228, ...), kind=kOutput, calls=%fused_computation | convolution fusion | flops 549453824 | bytes 14434304 | tf_op jit(solution)/shard_map/while/body/eval_jaxpr/cond/branch_1_fun/rgd,cd->rgc/dot_general | solution.py:12
  20.5 1.4 fusion.11
  21.9 1.3 convolution_add_fusion
  24.1 2.6 %collective-permute-start.3 = (f32[1024,128]{1,0:T(8,128)}, f32[1024,128]{1,0:T(8,128)S(1)}, u32[]{:S(2)}, u32[]{:S(2)}) collective-permute-start(f32[1024,128]{1,0:T(8,128)} %get-tuple-element.394), channel_id=1, source_target_pairs={{0,1},{1,2},{2,3},{3,4},{4,5},{5,6},{6,7},{7,0}} | collective-permute-start | bytes 1572872 | tf_op jit(solution)/shard_map/while/body/eval_jaxpr/ppermute | solution.py:46
  26.7 1.6 collective-permute-start.1
  28.3 5.5 %collective-permute-done.2 = f32[1024,128]{1,0:T(8,128)} collective-permute-done((f32[1024,128]{1,0:T(8,128)S(1)}, f32[1024,128]{1,0:T(8,128)}, u32[]{:S(2)}, u32[]{:S(2)}) %collective-permute-start.2) | collective-permute-done | bytes 524320 | tf_op jit(solution)/shard_map/while/body/eval_jaxpr/ppermute | solution.py:45
  33.8 1.0 copy.60
  34.9 4.6 %collective-permute-done.3 = f32[1024,128]{1,0:T(8,128)S(1)} collective-permute-done((f32[1024,128]{1,0:T(8,128)}, f32[1024,128]{1,0:T(8,128)S(1)}, u32[]{:S(2)}, u32[]{:S(2)}) %collective-permute-start.3) | collective-permute-done | bytes 524320 | tf_op jit(solution)/shard_map/while/body/eval_jaxpr/ppermute | solution.py:46
  40.3 2.0 collective-permute-done
  42.3 2.8 %collective-permute-done.1 = bf16[1024,128]{1,0:T(8,128)(2,1)S(1)} collective-permute-done((bf16[1024,128]{1,0:T(8,128)(2,1)}, bf16[1024,128]{1,0:T(8,128)(2,1)S(1)}, u32[]{:S(2)}, u32[]{:S(2)}) %collective-permute-start.1) | collective-permute-done | bytes 262176 | tf_op jit(solution)/shard_map/while/body/eval_jaxpr/ppermute | solution.py:44
  45.8 12.3 %collective-permute-start.2 = (f32[1024,128]{1,0:T(8,128)S(1)}, f32[1024,128]{1,0:T(8,128)}, u32[]{:S(2)}, u32[]{:S(2)}) collective-permute-start(f32[1024,128]{1,0:T(8,128)S(1)} %get-tuple-element.393), channel_id=1, source_target_pairs={{0,1},{1,2},{2,3},{3,4},{4,5},{5,6},{6,7},{7,0}} | collective-permute-start | bytes 1572872 | tf_op jit(solution)/shard_map/while/body/eval_jaxpr/ppermute | solution.py:45
  58.2 2.5 collective-permute-start.3
  60.7 2.5 collective-permute-start.1
  63.2 2.1 collective-permute-done.2
  65.3 1.0 copy.60
  66.4 4.6 %collective-permute-done.3 = f32[1024,128]{1,0:T(8,128)S(1)} collective-permute-done((f32[1024,128]{1,0:T(8,128)}, f32[1024,128]{1,0:T(8,128)S(1)}, u32[]{:S(2)}, u32[]{:S(2)}) %collective-permute-start.3) | collective-permute-done | bytes 524320 | tf_op jit(solution)/shard_map/while/body/eval_jaxpr/ppermute | solution.py:46
  71.7 2.0 collective-permute-done
  73.8 2.8 %collective-permute-done.1 = bf16[1024,128]{1,0:T(8,128)(2,1)S(1)} collective-permute-done((bf16[1024,128]{1,0:T(8,128)(2,1)}, bf16[1024,128]{1,0:T(8,128)(2,1)S(1)}, u32[]{:S(2)}, u32[]{:S(2)}) %collective-permute-start.1) | collective-permute-done | bytes 262176 | tf_op jit(solution)/shard_map/while/body/eval_jaxpr/ppermute | solution.py:44
  77.3 1.5 collective-permute-start.2
  78.8 15.9 %collective-permute-start.3 = (f32[1024,128]{1,0:T(8,128)}, f32[1024,128]{1,0:T(8,128)S(1)}, u32[]{:S(2)}, u32[]{:S(2)}) collective-permute-start(f32[1024,128]{1,0:T(8,128)} %get-tuple-element.394), channel_id=1, source_target_pairs={{0,1},{1,2},{2,3},{3,4},{4,5},{5,6},{6,7},{7,0}} | collective-permute-start | bytes 1572872 | tf_op jit(solution)/shard_map/while/body/eval_jaxpr/ppermute | solution.py:46
  94.7 3.4 %collective-permute-start.1 = (bf16[1024,128]{1,0:T(8,128)(2,1)}, bf16[1024,128]{1,0:T(8,128)(2,1)S(1)}, u32[]{:S(2)}, u32[]{:S(2)}) collective-permute-start(bf16[1024,128]{1,0:T(8,128)(2,1)} %copy.53), channel_id=1, source_target_pairs={{0,1},{1,2},{2,3},{3,4},{4,5},{5,6},{6,7},{7,0}} | collective-permute-start | bytes 786440 | tf_op jit(solution)/shard_map/while/body/eval_jaxpr/ppermute | solution.py:44
  98.1 1.0 copy.60
  99.1 3.3 %collective-permute-done.3 = f32[1024,128]{1,0:T(8,128)S(1)} collective-permute-done((f32[1024,128]{1,0:T(8,128)}, f32[1024,128]{1,0:T(8,128)S(1)}, u32[]{:S(2)}, u32[]{:S(2)}) %collective-permute-start.3) | collective-permute-done | bytes 524320 | tf_op jit(solution)/shard_map/while/body/eval_jaxpr/ppermute | solution.py:46
  103.2 2.0 collective-permute-done
  105.2 2.8 %collective-permute-done.1 = bf16[1024,128]{1,0:T(8,128)(2,1)S(1)} collective-permute-done((bf16[1024,128]{1,0:T(8,128)(2,1)}, bf16[1024,128]{1,0:T(8,128)(2,1)S(1)}, u32[]{:S(2)}, u32[]{:S(2)}) %collective-permute-start.1) | collective-permute-done | bytes 262176 | tf_op jit(solution)/shard_map/while/body/eval_jaxpr/ppermute | solution.py:44
  108.8 4.0 %collective-permute-start.2 = (f32[1024,128]{1,0:T(8,128)S(1)}, f32[1024,128]{1,0:T(8,128)}, u32[]{:S(2)}, u32[]{:S(2)}) collective-permute-start(f32[1024,128]{1,0:T(8,128)S(1)} %get-tuple-element.393), channel_id=1, source_target_pairs={{0,1},{1,2},{2,3},{3,4},{4,5},{5,6},{6,7},{7,0}} | collective-permute-start | bytes 1572872 | tf_op jit(solution)/shard_map/while/body/eval_jaxpr/ppermute | solution.py:45
  112.8 2.5 collective-permute-start.3
  115.3 14.3 %collective-permute-start = (bf16[1024,128]{1,0:T(8,128)(2,1)S(1)}, bf16[1024,128]{1,0:T(8,128)(2,1)S(1)}, u32[]{:S(2)}, u32[]{:S(2)}) collective-permute-start(bf16[1024,128]{1,0:T(8,128)(2,1)S(1)} %copy.52), channel_id=1, source_target_pairs={{0,1},{1,2},{2,3},{3,4},{4,5},{5,6},{6,7},{7,0}} | collective-permute-start | bytes 786440 | tf_op jit(solution)/shard_map/while/body/eval_jaxpr/ppermute | solution.py:43
  129.5 3.4 %collective-permute-start.1 = (bf16[1024,128]{1,0:T(8,128)(2,1)}, bf16[1024,128]{1,0:T(8,128)(2,1)S(1)}, u32[]{:S(2)}, u32[]{:S(2)}) collective-permute-start(bf16[1024,128]{1,0:T(8,128)(2,1)} %copy.53), channel_id=1, source_target_pairs={{0,1},{1,2},{2,3},{3,4},{4,5},{5,6},{6,7},{7,0}} | collective-permute-start | bytes 786440 | tf_op jit(solution)/shard_map/while/body/eval_jaxpr/ppermute | solution.py:44
  132.9 1.0 copy.60
  134.8 1.9 collective-permute-done
  136.7 2.8 %collective-permute-done.1 = bf16[1024,128]{1,0:T(8,128)(2,1)S(1)} collective-permute-done((bf16[1024,128]{1,0:T(8,128)(2,1)}, bf16[1024,128]{1,0:T(8,128)(2,1)S(1)}, u32[]{:S(2)}, u32[]{:S(2)}) %collective-permute-start.1) | collective-permute-done | bytes 262176 | tf_op jit(solution)/shard_map/while/body/eval_jaxpr/ppermute | solution.py:44
  140.3 1.7 collective-permute-start.2
  142.0 2.5 collective-permute-start.3
  144.5 6.5 %collective-permute-start = (bf16[1024,128]{1,0:T(8,128)(2,1)S(1)}, bf16[1024,128]{1,0:T(8,128)(2,1)S(1)}, u32[]{:S(2)}, u32[]{:S(2)}) collective-permute-start(bf16[1024,128]{1,0:T(8,128)(2,1)S(1)} %copy.52), channel_id=1, source_target_pairs={{0,1},{1,2},{2,3},{3,4},{4,5},{5,6},{6,7},{7,0}} | collective-permute-start | bytes 786440 | tf_op jit(solution)/shard_map/while/body/eval_jaxpr/ppermute | solution.py:43
  151.1 16.8 %collective-permute-start.1 = (bf16[1024,128]{1,0:T(8,128)(2,1)}, bf16[1024,128]{1,0:T(8,128)(2,1)S(1)}, u32[]{:S(2)}, u32[]{:S(2)}) collective-permute-start(bf16[1024,128]{1,0:T(8,128)(2,1)} %copy.53), channel_id=1, source_target_pairs={{0,1},{1,2},{2,3},{3,4},{4,5},{5,6},{6,7},{7,0}} | collective-permute-start | bytes 786440 | tf_op jit(solution)/shard_map/while/body/eval_jaxpr/ppermute | solution.py:44
  167.8 1.0 copy.60
  169.7 1.4 collective-permute-done.1
  171.8 2.9 %collective-permute-start.2 = (f32[1024,128]{1,0:T(8,128)S(1)}, f32[1024,128]{1,0:T(8,128)}, u32[]{:S(2)}, u32[]{:S(2)}) collective-permute-start(f32[1024,128]{1,0:T(8,128)S(1)} %get-tuple-element.393), channel_id=1, source_target_pairs={{0,1},{1,2},{2,3},{3,4},{4,5},{5,6},{6,7},{7,0}} | collective-permute-start | bytes 1572872 | tf_op jit(solution)/shard_map/while/body/eval_jaxpr/ppermute | solution.py:45
  174.7 2.5 collective-permute-start.3
  177.2 8.7 %collective-permute-start = (bf16[1024,128]{1,0:T(8,128)(2,1)S(1)}, bf16[1024,128]{1,0:T(8,128)(2,1)S(1)}, u32[]{:S(2)}, u32[]{:S(2)}) collective-permute-start(bf16[1024,128]{1,0:T(8,128)(2,1)S(1)} %copy.52), channel_id=1, source_target_pairs={{0,1},{1,2},{2,3},{3,4},{4,5},{5,6},{6,7},{7,0}} | collective-permute-start | bytes 786440 | tf_op jit(solution)/shard_map/while/body/eval_jaxpr/ppermute | solution.py:43
  185.9 3.4 %collective-permute-start.1 = (bf16[1024,128]{1,0:T(8,128)(2,1)}, bf16[1024,128]{1,0:T(8,128)(2,1)S(1)}, u32[]{:S(2)}, u32[]{:S(2)}) collective-permute-start(bf16[1024,128]{1,0:T(8,128)(2,1)} %copy.53), channel_id=1, source_target_pairs={{0,1},{1,2},{2,3},{3,4},{4,5},{5,6},{6,7},{7,0}} | collective-permute-start | bytes 786440 | tf_op jit(solution)/shard_map/while/body/eval_jaxpr/ppermute | solution.py:44
  189.3 1.9 collective-permute-done.2
  191.3 1.0 copy.60
  192.3 4.6 %collective-permute-done.3 = f32[1024,128]{1,0:T(8,128)S(1)} collective-permute-done((f32[1024,128]{1,0:T(8,128)}, f32[1024,128]{1,0:T(8,128)S(1)}, u32[]{:S(2)}, u32[]{:S(2)}) %collective-permute-start.3) | collective-permute-done | bytes 524320 | tf_op jit(solution)/shard_map/while/body/eval_jaxpr/ppermute | solution.py:46
  197.7 2.0 collective-permute-done
  199.7 2.8 %collective-permute-done.1 = bf16[1024,128]{1,0:T(8,128)(2,1)S(1)} collective-permute-done((bf16[1024,128]{1,0:T(8,128)(2,1)}, bf16[1024,128]{1,0:T(8,128)(2,1)S(1)}, u32[]{:S(2)}, u32[]{:S(2)}) %collective-permute-start.1) | collective-permute-done | bytes 262176 | tf_op jit(solution)/shard_map/while/body/eval_jaxpr/ppermute | solution.py:44
  203.9 5.9 %collective-permute-start = (bf16[1024,128]{1,0:T(8,128)(2,1)S(1)}, bf16[1024,128]{1,0:T(8,128)(2,1)S(1)}, u32[]{:S(2)}, u32[]{:S(2)}) collective-permute-start(bf16[1024,128]{1,0:T(8,128)(2,1)S(1)} %copy.52), channel_id=1, source_target_pairs={{0,1},{1,2},{2,3},{3,4},{4,5},{5,6},{6,7},{7,0}} | collective-permute-start | bytes 786440 | tf_op jit(solution)/shard_map/while/body/eval_jaxpr/ppermute | solution.py:43
  209.8 3.4 %collective-permute-start.1 = (bf16[1024,128]{1,0:T(8,128)(2,1)}, bf16[1024,128]{1,0:T(8,128)(2,1)S(1)}, u32[]{:S(2)}, u32[]{:S(2)}) collective-permute-start(bf16[1024,128]{1,0:T(8,128)(2,1)} %copy.53), channel_id=1, source_target_pairs={{0,1},{1,2},{2,3},{3,4},{4,5},{5,6},{6,7},{7,0}} | collective-permute-start | bytes 786440 | tf_op jit(solution)/shard_map/while/body/eval_jaxpr/ppermute | solution.py:44
  213.2 9.6 %collective-permute-done.2 = f32[1024,128]{1,0:T(8,128)} collective-permute-done((f32[1024,128]{1,0:T(8,128)S(1)}, f32[1024,128]{1,0:T(8,128)}, u32[]{:S(2)}, u32[]{:S(2)}) %collective-permute-start.2) | collective-permute-done | bytes 524320 | tf_op jit(solution)/shard_map/while/body/eval_jaxpr/ppermute | solution.py:45
  223.8 4.6 %collective-permute-done.3 = f32[1024,128]{1,0:T(8,128)S(1)} collective-permute-done((f32[1024,128]{1,0:T(8,128)}, f32[1024,128]{1,0:T(8,128)S(1)}, u32[]{:S(2)}, u32[]{:S(2)}) %collective-permute-start.3) | collective-permute-done | bytes 524320 | tf_op jit(solution)/shard_map/while/body/eval_jaxpr/ppermute | solution.py:46
  229.2 2.0 collective-permute-done
  231.2 2.8 %collective-permute-done.1 = bf16[1024,128]{1,0:T(8,128)(2,1)S(1)} collective-permute-done((bf16[1024,128]{1,0:T(8,128)(2,1)}, bf16[1024,128]{1,0:T(8,128)(2,1)S(1)}, u32[]{:S(2)}, u32[]{:S(2)}) %collective-permute-start.1) | collective-permute-done | bytes 262176 | tf_op jit(solution)/shard_map/while/body/eval_jaxpr/ppermute | solution.py:44
  235.0 1.1 convert.12
  236.1 1.6 collective-permute-start.5
  237.8 1.3 multiply_convert_fusion.2
  239.1 17.8 %collective-permute-done.5 = bf16[1024,128]{1,0:T(8,128)(2,1)S(1)} collective-permute-done((bf16[1024,128]{1,0:T(8,128)(2,1)S(1)}, bf16[1024,128]{1,0:T(8,128)(2,1)S(1)}, u32[]{:S(2)}, u32[]{:S(2)}) %collective-permute-start.5) | collective-permute-done | bytes 262176 | tf_op jit(solution)/shard_map/ppermute | solution.py:54
  (55 shorter events, 20.0 us)
Async XLA Ops:
  9.8 1.6 copy-start.2
  23.2 10.6 %collective-permute-start.2 = (f32[1024,128]{1,0:T(8,128)S(1)}, f32[1024,128]{1,0:T(8,128)}, u32[]{:S(2)}, u32[]{:S(2)}) collective-permute-start(f32[1024,128]{1,0:T(8,128)S(1)} %get-tuple-element.393), channel_id=1, source_target_pairs={{0,1},{1,2},{2,3},{3,4},{4,5},{5,6},{6,7},{7,0}} | collective-permute-start | bytes 1572872 | tf_op jit(solution)/shard_map/while/body/eval_jaxpr/ppermute | solution.py:45
  24.1 15.4 %collective-permute-start.3 = (f32[1024,128]{1,0:T(8,128)}, f32[1024,128]{1,0:T(8,128)S(1)}, u32[]{:S(2)}, u32[]{:S(2)}) collective-permute-start(f32[1024,128]{1,0:T(8,128)} %get-tuple-element.394), channel_id=1, source_target_pairs={{0,1},{1,2},{2,3},{3,4},{4,5},{5,6},{6,7},{7,0}} | collective-permute-start | bytes 1572872 | tf_op jit(solution)/shard_map/while/body/eval_jaxpr/ppermute | solution.py:46
  26.7 15.6 %collective-permute-start = (bf16[1024,128]{1,0:T(8,128)(2,1)S(1)}, bf16[1024,128]{1,0:T(8,128)(2,1)S(1)}, u32[]{:S(2)}, u32[]{:S(2)}) collective-permute-start(bf16[1024,128]{1,0:T(8,128)(2,1)S(1)} %copy.52), channel_id=1, source_target_pairs={{0,1},{1,2},{2,3},{3,4},{4,5},{5,6},{6,7},{7,0}} | collective-permute-start | bytes 786440 | tf_op jit(solution)/shard_map/while/body/eval_jaxpr/ppermute | solution.py:43
  26.7 18.3 %collective-permute-start.1 = (bf16[1024,128]{1,0:T(8,128)(2,1)}, bf16[1024,128]{1,0:T(8,128)(2,1)S(1)}, u32[]{:S(2)}, u32[]{:S(2)}) collective-permute-start(bf16[1024,128]{1,0:T(8,128)(2,1)} %copy.53), channel_id=1, source_target_pairs={{0,1},{1,2},{2,3},{3,4},{4,5},{5,6},{6,7},{7,0}} | collective-permute-start | bytes 786440 | tf_op jit(solution)/shard_map/while/body/eval_jaxpr/ppermute | solution.py:44
  45.8 19.5 %collective-permute-start.2 = (f32[1024,128]{1,0:T(8,128)S(1)}, f32[1024,128]{1,0:T(8,128)}, u32[]{:S(2)}, u32[]{:S(2)}) collective-permute-start(f32[1024,128]{1,0:T(8,128)S(1)} %get-tuple-element.393), channel_id=1, source_target_pairs={{0,1},{1,2},{2,3},{3,4},{4,5},{5,6},{6,7},{7,0}} | collective-permute-start | bytes 1572872 | tf_op jit(solution)/shard_map/while/body/eval_jaxpr/ppermute | solution.py:45
  58.2 12.8 %collective-permute-start.3 = (f32[1024,128]{1,0:T(8,128)}, f32[1024,128]{1,0:T(8,128)S(1)}, u32[]{:S(2)}, u32[]{:S(2)}) collective-permute-start(f32[1024,128]{1,0:T(8,128)} %get-tuple-element.394), channel_id=1, source_target_pairs={{0,1},{1,2},{2,3},{3,4},{4,5},{5,6},{6,7},{7,0}} | collective-permute-start | bytes 1572872 | tf_op jit(solution)/shard_map/while/body/eval_jaxpr/ppermute | solution.py:46
  60.7 13.1 %collective-permute-start = (bf16[1024,128]{1,0:T(8,128)(2,1)S(1)}, bf16[1024,128]{1,0:T(8,128)(2,1)S(1)}, u32[]{:S(2)}, u32[]{:S(2)}) collective-permute-start(bf16[1024,128]{1,0:T(8,128)(2,1)S(1)} %copy.52), channel_id=1, source_target_pairs={{0,1},{1,2},{2,3},{3,4},{4,5},{5,6},{6,7},{7,0}} | collective-permute-start | bytes 786440 | tf_op jit(solution)/shard_map/while/body/eval_jaxpr/ppermute | solution.py:43
  60.7 15.8 %collective-permute-start.1 = (bf16[1024,128]{1,0:T(8,128)(2,1)}, bf16[1024,128]{1,0:T(8,128)(2,1)S(1)}, u32[]{:S(2)}, u32[]{:S(2)}) collective-permute-start(bf16[1024,128]{1,0:T(8,128)(2,1)} %copy.53), channel_id=1, source_target_pairs={{0,1},{1,2},{2,3},{3,4},{4,5},{5,6},{6,7},{7,0}} | collective-permute-start | bytes 786440 | tf_op jit(solution)/shard_map/while/body/eval_jaxpr/ppermute | solution.py:44
  77.3 20.8 %collective-permute-start.2 = (f32[1024,128]{1,0:T(8,128)S(1)}, f32[1024,128]{1,0:T(8,128)}, u32[]{:S(2)}, u32[]{:S(2)}) collective-permute-start(f32[1024,128]{1,0:T(8,128)S(1)} %get-tuple-element.393), channel_id=1, source_target_pairs={{0,1},{1,2},{2,3},{3,4},{4,5},{5,6},{6,7},{7,0}} | collective-permute-start | bytes 1572872 | tf_op jit(solution)/shard_map/while/body/eval_jaxpr/ppermute | solution.py:45
  78.8 23.6 %collective-permute-start.3 = (f32[1024,128]{1,0:T(8,128)}, f32[1024,128]{1,0:T(8,128)S(1)}, u32[]{:S(2)}, u32[]{:S(2)}) collective-permute-start(f32[1024,128]{1,0:T(8,128)} %get-tuple-element.394), channel_id=1, source_target_pairs={{0,1},{1,2},{2,3},{3,4},{4,5},{5,6},{6,7},{7,0}} | collective-permute-start | bytes 1572872 | tf_op jit(solution)/shard_map/while/body/eval_jaxpr/ppermute | solution.py:46
  94.7 10.6 %collective-permute-start = (bf16[1024,128]{1,0:T(8,128)(2,1)S(1)}, bf16[1024,128]{1,0:T(8,128)(2,1)S(1)}, u32[]{:S(2)}, u32[]{:S(2)}) collective-permute-start(bf16[1024,128]{1,0:T(8,128)(2,1)S(1)} %copy.52), channel_id=1, source_target_pairs={{0,1},{1,2},{2,3},{3,4},{4,5},{5,6},{6,7},{7,0}} | collective-permute-start | bytes 786440 | tf_op jit(solution)/shard_map/while/body/eval_jaxpr/ppermute | solution.py:43
  94.7 13.4 %collective-permute-start.1 = (bf16[1024,128]{1,0:T(8,128)(2,1)}, bf16[1024,128]{1,0:T(8,128)(2,1)S(1)}, u32[]{:S(2)}, u32[]{:S(2)}) collective-permute-start(bf16[1024,128]{1,0:T(8,128)(2,1)} %copy.53), channel_id=1, source_target_pairs={{0,1},{1,2},{2,3},{3,4},{4,5},{5,6},{6,7},{7,0}} | collective-permute-start | bytes 786440 | tf_op jit(solution)/shard_map/while/body/eval_jaxpr/ppermute | solution.py:44
  108.8 24.1 %collective-permute-start.2 = (f32[1024,128]{1,0:T(8,128)S(1)}, f32[1024,128]{1,0:T(8,128)}, u32[]{:S(2)}, u32[]{:S(2)}) collective-permute-start(f32[1024,128]{1,0:T(8,128)S(1)} %get-tuple-element.393), channel_id=1, source_target_pairs={{0,1},{1,2},{2,3},{3,4},{4,5},{5,6},{6,7},{7,0}} | collective-permute-start | bytes 1572872 | tf_op jit(solution)/shard_map/while/body/eval_jaxpr/ppermute | solution.py:45
  112.8 21.2 %collective-permute-start.3 = (f32[1024,128]{1,0:T(8,128)}, f32[1024,128]{1,0:T(8,128)S(1)}, u32[]{:S(2)}, u32[]{:S(2)}) collective-permute-start(f32[1024,128]{1,0:T(8,128)} %get-tuple-element.394), channel_id=1, source_target_pairs={{0,1},{1,2},{2,3},{3,4},{4,5},{5,6},{6,7},{7,0}} | collective-permute-start | bytes 1572872 | tf_op jit(solution)/shard_map/while/body/eval_jaxpr/ppermute | solution.py:46
  115.3 21.5 %collective-permute-start = (bf16[1024,128]{1,0:T(8,128)(2,1)S(1)}, bf16[1024,128]{1,0:T(8,128)(2,1)S(1)}, u32[]{:S(2)}, u32[]{:S(2)}) collective-permute-start(bf16[1024,128]{1,0:T(8,128)(2,1)S(1)} %copy.52), channel_id=1, source_target_pairs={{0,1},{1,2},{2,3},{3,4},{4,5},{5,6},{6,7},{7,0}} | collective-permute-start | bytes 786440 | tf_op jit(solution)/shard_map/while/body/eval_jaxpr/ppermute | solution.py:43
  129.5 10.0 %collective-permute-start.1 = (bf16[1024,128]{1,0:T(8,128)(2,1)}, bf16[1024,128]{1,0:T(8,128)(2,1)S(1)}, u32[]{:S(2)}, u32[]{:S(2)}) collective-permute-start(bf16[1024,128]{1,0:T(8,128)(2,1)} %copy.53), channel_id=1, source_target_pairs={{0,1},{1,2},{2,3},{3,4},{4,5},{5,6},{6,7},{7,0}} | collective-permute-start | bytes 786440 | tf_op jit(solution)/shard_map/while/body/eval_jaxpr/ppermute | solution.py:44
  140.3 27.5 %collective-permute-start.2 = (f32[1024,128]{1,0:T(8,128)S(1)}, f32[1024,128]{1,0:T(8,128)}, u32[]{:S(2)}, u32[]{:S(2)}) collective-permute-start(f32[1024,128]{1,0:T(8,128)S(1)} %get-tuple-element.393), channel_id=1, source_target_pairs={{0,1},{1,2},{2,3},{3,4},{4,5},{5,6},{6,7},{7,0}} | collective-permute-start | bytes 1572872 | tf_op jit(solution)/shard_map/while/body/eval_jaxpr/ppermute | solution.py:45
  142.0 26.8 %collective-permute-start.3 = (f32[1024,128]{1,0:T(8,128)}, f32[1024,128]{1,0:T(8,128)S(1)}, u32[]{:S(2)}, u32[]{:S(2)}) collective-permute-start(f32[1024,128]{1,0:T(8,128)} %get-tuple-element.394), channel_id=1, source_target_pairs={{0,1},{1,2},{2,3},{3,4},{4,5},{5,6},{6,7},{7,0}} | collective-permute-start | bytes 1572872 | tf_op jit(solution)/shard_map/while/body/eval_jaxpr/ppermute | solution.py:46
  144.5 25.1 %collective-permute-start = (bf16[1024,128]{1,0:T(8,128)(2,1)S(1)}, bf16[1024,128]{1,0:T(8,128)(2,1)S(1)}, u32[]{:S(2)}, u32[]{:S(2)}) collective-permute-start(bf16[1024,128]{1,0:T(8,128)(2,1)S(1)} %copy.52), channel_id=1, source_target_pairs={{0,1},{1,2},{2,3},{3,4},{4,5},{5,6},{6,7},{7,0}} | collective-permute-start | bytes 786440 | tf_op jit(solution)/shard_map/while/body/eval_jaxpr/ppermute | solution.py:43
  151.1 20.0 %collective-permute-start.1 = (bf16[1024,128]{1,0:T(8,128)(2,1)}, bf16[1024,128]{1,0:T(8,128)(2,1)S(1)}, u32[]{:S(2)}, u32[]{:S(2)}) collective-permute-start(bf16[1024,128]{1,0:T(8,128)(2,1)} %copy.53), channel_id=1, source_target_pairs={{0,1},{1,2},{2,3},{3,4},{4,5},{5,6},{6,7},{7,0}} | collective-permute-start | bytes 786440 | tf_op jit(solution)/shard_map/while/body/eval_jaxpr/ppermute | solution.py:44
  171.8 19.5 %collective-permute-start.2 = (f32[1024,128]{1,0:T(8,128)S(1)}, f32[1024,128]{1,0:T(8,128)}, u32[]{:S(2)}, u32[]{:S(2)}) collective-permute-start(f32[1024,128]{1,0:T(8,128)S(1)} %get-tuple-element.393), channel_id=1, source_target_pairs={{0,1},{1,2},{2,3},{3,4},{4,5},{5,6},{6,7},{7,0}} | collective-permute-start | bytes 1572872 | tf_op jit(solution)/shard_map/while/body/eval_jaxpr/ppermute | solution.py:45
  174.7 22.2 %collective-permute-start.3 = (f32[1024,128]{1,0:T(8,128)}, f32[1024,128]{1,0:T(8,128)S(1)}, u32[]{:S(2)}, u32[]{:S(2)}) collective-permute-start(f32[1024,128]{1,0:T(8,128)} %get-tuple-element.394), channel_id=1, source_target_pairs={{0,1},{1,2},{2,3},{3,4},{4,5},{5,6},{6,7},{7,0}} | collective-permute-start | bytes 1572872 | tf_op jit(solution)/shard_map/while/body/eval_jaxpr/ppermute | solution.py:46
  177.2 22.5 %collective-permute-start = (bf16[1024,128]{1,0:T(8,128)(2,1)S(1)}, bf16[1024,128]{1,0:T(8,128)(2,1)S(1)}, u32[]{:S(2)}, u32[]{:S(2)}) collective-permute-start(bf16[1024,128]{1,0:T(8,128)(2,1)S(1)} %copy.52), channel_id=1, source_target_pairs={{0,1},{1,2},{2,3},{3,4},{4,5},{5,6},{6,7},{7,0}} | collective-permute-start | bytes 786440 | tf_op jit(solution)/shard_map/while/body/eval_jaxpr/ppermute | solution.py:43
  185.9 16.6 %collective-permute-start.1 = (bf16[1024,128]{1,0:T(8,128)(2,1)}, bf16[1024,128]{1,0:T(8,128)(2,1)S(1)}, u32[]{:S(2)}, u32[]{:S(2)}) collective-permute-start(bf16[1024,128]{1,0:T(8,128)(2,1)} %copy.53), channel_id=1, source_target_pairs={{0,1},{1,2},{2,3},{3,4},{4,5},{5,6},{6,7},{7,0}} | collective-permute-start | bytes 786440 | tf_op jit(solution)/shard_map/while/body/eval_jaxpr/ppermute | solution.py:44
  203.3 19.5 %collective-permute-start.2 = (f32[1024,128]{1,0:T(8,128)S(1)}, f32[1024,128]{1,0:T(8,128)}, u32[]{:S(2)}, u32[]{:S(2)}) collective-permute-start(f32[1024,128]{1,0:T(8,128)S(1)} %get-tuple-element.393), channel_id=1, source_target_pairs={{0,1},{1,2},{2,3},{3,4},{4,5},{5,6},{6,7},{7,0}} | collective-permute-start | bytes 1572872 | tf_op jit(solution)/shard_map/while/body/eval_jaxpr/ppermute | solution.py:45
  203.3 25.1 %collective-permute-start.3 = (f32[1024,128]{1,0:T(8,128)}, f32[1024,128]{1,0:T(8,128)S(1)}, u32[]{:S(2)}, u32[]{:S(2)}) collective-permute-start(f32[1024,128]{1,0:T(8,128)} %get-tuple-element.394), channel_id=1, source_target_pairs={{0,1},{1,2},{2,3},{3,4},{4,5},{5,6},{6,7},{7,0}} | collective-permute-start | bytes 1572872 | tf_op jit(solution)/shard_map/while/body/eval_jaxpr/ppermute | solution.py:46
  203.9 27.3 %collective-permute-start = (bf16[1024,128]{1,0:T(8,128)(2,1)S(1)}, bf16[1024,128]{1,0:T(8,128)(2,1)S(1)}, u32[]{:S(2)}, u32[]{:S(2)}) collective-permute-start(bf16[1024,128]{1,0:T(8,128)(2,1)S(1)} %copy.52), channel_id=1, source_target_pairs={{0,1},{1,2},{2,3},{3,4},{4,5},{5,6},{6,7},{7,0}} | collective-permute-start | bytes 786440 | tf_op jit(solution)/shard_map/while/body/eval_jaxpr/ppermute | solution.py:43
  209.8 24.2 %collective-permute-start.1 = (bf16[1024,128]{1,0:T(8,128)(2,1)}, bf16[1024,128]{1,0:T(8,128)(2,1)S(1)}, u32[]{:S(2)}, u32[]{:S(2)}) collective-permute-start(bf16[1024,128]{1,0:T(8,128)(2,1)} %copy.53), channel_id=1, source_target_pairs={{0,1},{1,2},{2,3},{3,4},{4,5},{5,6},{6,7},{7,0}} | collective-permute-start | bytes 786440 | tf_op jit(solution)/shard_map/while/body/eval_jaxpr/ppermute | solution.py:44
  235.0 21.9 %collective-permute-start.4 = (f32[1024,128]{1,0:T(8,128)S(1)}, f32[1024,128]{1,0:T(8,128)S(1)}, u32[]{:S(2)}, u32[]{:S(2)}) collective-permute-start(f32[1024,128]{1,0:T(8,128)S(1)} %get-tuple-element.274), channel_id=1, source_target_pairs={{0,1},{1,2},{2,3},{3,4},{4,5},{5,6},{6,7},{7,0}} | collective-permute-start | bytes 1572872 | tf_op jit(solution)/shard_map/ppermute | solution.py:53
  236.1 20.8 %collective-permute-start.5 = (bf16[1024,128]{1,0:T(8,128)(2,1)S(1)}, bf16[1024,128]{1,0:T(8,128)(2,1)S(1)}, u32[]{:S(2)}, u32[]{:S(2)}) collective-permute-start(bf16[1024,128]{1,0:T(8,128)(2,1)S(1)} %convert.12), channel_id=1, source_target_pairs={{0,1},{1,2},{2,3},{3,4},{4,5},{5,6},{6,7},{7,0}} | collective-permute-start | bytes 786440 | tf_op jit(solution)/shard_map/ppermute | solution.py:54
where the time goes:
time: 262 us; the launch traced here: 258 us
  starting transfers between devices  124 us (47%)
  waiting for transfers between devices  88.9 us (34%)
  local copies, waits for them, and re-layouts  25.5 us (10%)
  matrix products  13 us (5%)
  other arithmetic  5.87 us (2%)
    ppermute x7, starting transfers between devices, step_fn(): k_next = lax.ppermute(k_cur, 'cp', forward_perm)  35.6 us
    ppermute x7, starting transfers between devices, step_fn(): v_next = lax.ppermute(v_cur, 'cp', forward_perm)  34.4 us
    ppermute x7, starting transfers between devices, step_fn(): dv_next = lax.ppermute(dv_acc, 'cp', forward_perm)  29 us
    ppermute x7, starting transfers between devices, step_fn(): dk_next = lax.ppermute(dk_acc, 'cp', forward_perm)  23.4 us
    ppermute x7, waiting for transfers between devices, step_fn(): dv_next = lax.ppermute(dv_acc, 'cp', forward_perm)  21.6 us
    ppermute x7, waiting for transfers between devices, step_fn(): dk_next = lax.ppermute(dk_acc, 'cp', forward_perm)  19.2 us
    ppermute x7, waiting for transfers between devices, step_fn(): v_next = lax.ppermute(v_cur, 'cp', forward_perm)  18.2 us
    ppermute x1, waiting for transfers between devices, local_fn(): dv_home = lax.ppermute(dv_acc, 'cp', forward_perm)  17.8 us
  transfers between devices with their start and end apart: 30, of which 23 were waited for; matrix products, arithmetic and copies ran while one was open for 6% of the time, Pallas kernels for 0%

commit v1 on v0

v1 whole, which is shorter than its diff:
```python
import functools
import math

import jax
import jax.numpy as jnp
from jax import lax
from jax.experimental import pallas as pl
from jax.experimental.pallas import tpu as pltpu
from jax.sharding import PartitionSpec as P

BF16, F32 = jnp.bfloat16, jnp.float32
NT = (((1,), (1,)), ((), ()))
CHUNKS = 4
COLS = 256


def dot(a, b):
    return jnp.dot(a, b, preferred_element_type=F32)


def dot_nt(a, b):
    return lax.dot_general(a, b, NT, preferred_element_type=F32)


def kernel(rows, keys, head, q_hbm, k_hbm, v_hbm, o_hbm, do_hbm, lse_hbm, dq_ref, dk_ref, dv_ref,
           qbuf, kvbuf, obuf, auxr, own_aux, chunk_aux, k_one, v_one, q_t, do_t, dq_acc, dk_t, dv_t,
           stage_sem, recv_sem, aux_recv, own_send, own_aux_send, pair_send, pair_aux_send,
           x_send, y_send, x_aux_send):
    me = lax.axis_index('cp')
    core, px, py = me % 2, (me // 2) % 2, me // 4
    pair = me + 1 - 2 * core
    nx = me + 2 - 4 * px
    ny = me + 4 - 8 * py
    diag = nx + 4 - 8 * py
    other = pair - me
    mid = (px + py) == 1
    qc, kc = rows // CHUNKS, keys // CHUNKS
    scale = head ** -0.5
    exp_scale = scale * math.log2(math.e)

    def q_copy(slot, n, dest, send, recv):
        part = pl.ds(n * qc, qc)
        return pltpu.make_async_remote_copy(
            qbuf.at[slot, :, part], qbuf.at[slot, :, part], send, recv,
            device_id={'cp': dest}, device_id_type=pl.DeviceIdType.MESH)

    def kv_copy(slot, n, dest, send, recv):
        part = pl.ds(n * kc, kc)
        return pltpu.make_async_remote_copy(
            kvbuf.at[slot, :, part], kvbuf.at[slot, :, part], send, recv,
            device_id={'cp': dest}, device_id_type=pl.DeviceIdType.MESH)

    def aux_copy(slot, dest, send):
        return pltpu.make_async_remote_copy(
            auxr.at[slot], auxr.at[slot], send, aux_recv.at[slot],
            device_id={'cp': dest}, device_id_type=pl.DeviceIdType.MESH)

    stages = [
        pltpu.make_async_copy(k_hbm, kvbuf.at[me, 0], stage_sem.at[0]),
        pltpu.make_async_copy(v_hbm, kvbuf.at[me, 1], stage_sem.at[1]),
        pltpu.make_async_copy(q_hbm, qbuf.at[me, 0], stage_sem.at[2]),
        pltpu.make_async_copy(do_hbm, qbuf.at[me, 1], stage_sem.at[3]),
        pltpu.make_async_copy(o_hbm, obuf, stage_sem.at[4]),
        pltpu.make_async_copy(lse_hbm, auxr.at[me, :, pl.ds(0, 4)], stage_sem.at[5]),
    ]
    for s in stages:
        s.start()

    barrier = pltpu.get_barrier_semaphore()
    for dest in (pair, nx, ny):
        pl.semaphore_signal(barrier, inc=1, device_id={'cp': dest}, device_id_type=pl.DeviceIdType.MESH)
    pl.semaphore_wait(barrier, 3)

    def order(d, n):
        return (n + 2) % CHUNKS if d == 1 else n

    dests = (pair, nx, ny)
    for s in stages[:4]:
        s.wait()
    for d, dest in enumerate(dests):
        @pl.when(dest > me)
        def _():
            for n in range(CHUNKS):
                c = order(d, n)
                kv_copy(me, c, dest, own_send.at[d, c], recv_sem.at[me, c]).start()

        @pl.when(dest < me)
        def _():
            c = order(d, 0)
            q_copy(me, c, dest, own_send.at[d, c], recv_sem.at[me, c]).start()

    lane = lax.broadcasted_iota(jnp.int32, (COLS, head), 1)
    k_one[...] = jnp.where(lane < 3, -1.0, 0.0).astype(BF16)
    v_one[...] = jnp.where((lane >= 3) & (lane < 6), -1.0, 0.0).astype(BF16)
    dq_acc[...] = jnp.zeros_like(dq_acc)
    dk_t[...] = jnp.zeros_like(dk_t)
    dv_t[...] = jnp.zeros_like(dv_t)
    for s in stages[4:]:
        s.wait()

    def delta_rows(n, _):
        auxr[me, n, 0:4] = auxr[me, n, 0:4] * (1.0 / scale)
        for g in range(qc // 128):
            part = pl.ds(pl.multiple_of(n * qc + g * 128, 128), 128)
            d = jnp.sum(qbuf[me, 1, part].astype(F32) * obuf[part].astype(F32), axis=1, keepdims=True)
            auxr[me, n, 4 + g:5 + g] = jnp.transpose(jnp.broadcast_to(d, (128, 128)))[0:1]
        return 0

    lax.fori_loop(0, CHUNKS, delta_rows, 0)

    def fill_aux(slot, n, dst, base):
        a = auxr[slot, n]
        hi = a.astype(BF16).astype(F32)
        r = a - hi
        md = r.astype(BF16).astype(F32)
        lo = r - md
        sub = lax.broadcasted_iota(jnp.int32, (8, 128), 0)
        for g in range(qc // 128):
            m = jnp.zeros((8, 128), F32)
            for i, row in enumerate((hi[g:g + 1], md[g:g + 1], lo[g:g + 1],
                                     hi[4 + g:5 + g], md[4 + g:5 + g], lo[4 + g:5 + g])):
                m = jnp.where(sub == i, row, m)
            m = jnp.concatenate([m, jnp.zeros((120, 128), F32)], axis=0)
            dst[pl.ds(base + g * 128, 128)] = jnp.transpose(m).astype(BF16)

    def own_fill(n, _):
        fill_aux(me, n, own_aux, pl.multiple_of(n * qc, 128))
        return 0

    lax.fori_loop(0, CHUNKS, own_fill, 0)

    def scores(q, do, aux, k, v):
        s = dot_nt(jnp.concatenate([q, aux], axis=1), jnp.concatenate([k, k_one[...]], axis=1))
        p = jnp.exp2(s * exp_scale)
        d = dot_nt(jnp.concatenate([do, aux], axis=1), jnp.concatenate([v, v_one[...]], axis=1))
        return p, d

    for rb in range(CHUNKS):
        rpart = pl.ds(rb * qc, qc)
        q, do, aux = qbuf[me, 0, rpart], qbuf[me, 1, rpart], own_aux[rpart]
        qt, dot_ = jnp.transpose(q), jnp.transpose(do)
        dq = None
        for cb in range(rb + 1):
            cpart = pl.ds(cb * kc, kc)
            k, v = kvbuf[me, 0, cpart], kvbuf[me, 1, cpart]
            p, d = scores(q, do, aux, k, v)
            if cb == rb:
                row = lax.broadcasted_iota(jnp.int32, (qc, kc), 0)
                col = lax.broadcasted_iota(jnp.int32, (qc, kc), 1)
                p = jnp.where(2 * col <= row, p, 0.0)
            ds = (p * d).astype(BF16)
            dv_t[:, cpart] += dot(dot_, p.astype(BF16))
            dk_t[:, cpart] += dot(qt, ds)
            term = dot(ds, k)
            dq = term if dq is None else dq + term
        dq_acc[rpart] = dq

    for d, dest in enumerate(dests):
        @pl.when(dest < me)
        def _():
            aux_copy(me, dest, own_aux_send.at[d]).start()
            for n in range(1, CHUNKS):
                c = order(d, n)
                q_copy(me, c, dest, own_send.at[d, c], recv_sem.at[me, c]).start()

    def plan(t):
        ta, tb = t - 4, t - 20
        na, ka = ta // 4, ta % 4
        nb, kb = tb // 2, tb % 2
        first, second = t < 4, t < 20
        dn = jnp.where(mid, nb, (nb % 2) * 2 + nb // 2)
        n = jnp.where(first, t, jnp.where(second, na, nb))
        src_a = jnp.where(ka % 2 == 0, nx, ny) + jnp.where(ka >= 2, other, 0)
        src_b = diag + jnp.where(kb == 1, other, 0)
        src = jnp.where(first, pair, jnp.where(second, src_a, src_b))
        pa = jnp.where(ka % 2 == 0, (na + 2) % CHUNKS, na)
        piece = jnp.where(first, t, jnp.where(second, pa, dn))
        stream = jnp.where(first, 3, jnp.where(second, jnp.where(ka < 2, ka, 3), jnp.where(kb == 0, 2, 3)))
        return stream, src, piece, n

    def forwards(stream, piece):
        to_pair = stream < 3
        to_x = (stream == 1) & (jnp.logical_not(mid) | (piece < 2))
        to_y = (stream == 0) & mid & (piece >= 2)
        return to_pair, to_x, to_y

    def step(t, _):
        stream, src, piece, n = plan(t)
        to_pair, to_x, to_y = forwards(stream, piece)
        idx = jnp.minimum(stream, 2)
        recv = recv_sem.at[src, piece]

        @pl.when(src > me)
        def _():
            @pl.when(n == 0)
            def _():
                aux_copy(src, me, own_aux_send.at[0]).wait_recv()

                @pl.when(to_pair)
                def _():
                    aux_copy(src, pair, pair_aux_send.at[idx]).start()

                @pl.when(to_x)
                def _():
                    aux_copy(src, nx, x_aux_send).start()

            q_copy(src, piece, me, x_send.at[piece], recv).wait_recv()

            @pl.when(to_x)
            def _():
                q_copy(src, piece, nx, x_send.at[piece], recv).start()

            @pl.when(to_y)
            def _():
                q_copy(src, piece, ny, y_send.at[piece], recv).start()

            @pl.when(to_pair)
            def _():
                q_copy(src, piece, pair, pair_send.at[idx, piece], recv).start()

            fill_aux(src, piece, chunk_aux, 0)
            rpart = pl.ds(pl.multiple_of(piece * qc, qc), qc)
            q, do, aux = qbuf[src, 0, rpart], qbuf[src, 1, rpart], chunk_aux[...]
            q_t[...] = jnp.transpose(q)
            do_t[...] = jnp.transpose(do)
            for cb in range(keys // COLS):
                cpart = pl.ds(cb * COLS, COLS)
                p, d = scores(q, do, aux, kvbuf[me, 0, cpart], kvbuf[me, 1, cpart])
                ds = (p * d).astype(BF16)
                dv_t[:, cpart] += dot(do_t[...], p.astype(BF16))
                dk_t[:, cpart] += dot(q_t[...], ds)

        @pl.when(src < me)
        def _():
            kv_copy(src, piece, me, x_send.at[piece], recv).wait_recv()

            @pl.when(to_x)
            def _():
                kv_copy(src, piece, nx, x_send.at[piece], recv).start()

            @pl.when(to_y)
            def _():
                kv_copy(src, piece, ny, y_send.at[piece], recv).start()

            @pl.when(to_pair)
            def _():
                kv_copy(src, piece, pair, pair_send.at[idx, piece], recv).start()

            cpart = pl.ds(pl.multiple_of(piece * kc, kc), kc)
            k, v = kvbuf[src, 0, cpart], kvbuf[src, 1, cpart]
            for rb in range(CHUNKS):
                rpart = pl.ds(rb * qc, qc)
                p, d = scores(qbuf[me, 0, rpart], qbuf[me, 1, rpart], own_aux[rpart], k, v)
                ds = (p * d).astype(BF16)
                dq_acc[rpart] += dot(ds, k)

        return 0

    lax.fori_loop(0, 28, step, 0)

    dq_ref[...] = (dq_acc[...] * scale).astype(BF16)
    dk_ref[...] = (jnp.transpose(dk_t[...]) * scale).astype(BF16)
    dv_ref[...] = jnp.transpose(dv_t[...]).astype(BF16)

    for d, dest in enumerate(dests):
        @pl.when(dest > me)
        def _():
            for c in range(CHUNKS):
                kv_copy(me, c, dest, own_send.at[d, c], recv_sem.at[me, c]).wait_send()

        @pl.when(dest < me)
        def _():
            aux_copy(me, dest, own_aux_send.at[d]).wait_send()
            for c in range(CHUNKS):
                q_copy(me, c, dest, own_send.at[d, c], recv_sem.at[me, c]).wait_send()

    def drain(t, _):
        stream, src, piece, n = plan(t)
        to_pair, to_x, to_y = forwards(stream, piece)
        idx = jnp.minimum(stream, 2)
        recv = recv_sem.at[src, piece]
        for make, is_q in ((q_copy, True), (kv_copy, False)):
            @pl.when((src > me) if is_q else (src < me))
            def _():
                @pl.when(to_x)
                def _():
                    make(src, piece, nx, x_send.at[piece], recv).wait_send()

                @pl.when(to_y)
                def _():
                    make(src, piece, ny, y_send.at[piece], recv).wait_send()

                @pl.when(to_pair)
                def _():
                    make(src, piece, pair, pair_send.at[idx, piece], recv).wait_send()

                if is_q:
                    @pl.when((n == 0) & to_pair)
                    def _():
                        aux_copy(src, pair, pair_aux_send.at[idx]).wait_send()

                    @pl.when((n == 0) & to_x)
                    def _():
                        aux_copy(src, nx, x_aux_send).wait_send()
        return 0

    lax.fori_loop(4, 28, drain, 0)


def solution(mesh):
    n_dev = mesh.shape['cp']
    row_spec = P(('dp', 'cp'))

    def local_fn(q_tok, k_tok, v_tok, fwd_out, d_out, lse_row):
        tokens, groups, head = q_tok.shape
        rows = tokens * groups
        flat = lambda x: x.reshape(rows, head)
        lse = lse_row.reshape(CHUNKS, rows // CHUNKS // 128, 128)
        dma = pltpu.SemaphoreType.DMA
        grad_q, grad_k, grad_v = pl.pallas_call(
            functools.partial(kernel, rows, tokens, head),
            out_shape=(jax.ShapeDtypeStruct((rows, head), BF16),
                       jax.ShapeDtypeStruct((tokens, head), BF16),
                       jax.ShapeDtypeStruct((tokens, head), BF16)),
            in_specs=[pl.BlockSpec(memory_space=pl.ANY)] * 6,
            out_specs=(pl.BlockSpec(memory_space=pltpu.VMEM),) * 3,
            scratch_shapes=[
                pltpu.VMEM((n_dev, 2, rows, head), BF16),
                pltpu.VMEM((n_dev, 2, tokens, head), BF16),
                pltpu.VMEM((rows, head), BF16),
                pltpu.VMEM((n_dev, CHUNKS, 8, 128), F32),
                pltpu.VMEM((rows, head), BF16),
                pltpu.VMEM((rows // CHUNKS, head), BF16),
                pltpu.VMEM((COLS, head), BF16),
                pltpu.VMEM((COLS, head), BF16),
                pltpu.VMEM((head, rows // CHUNKS), BF16),
                pltpu.VMEM((head, rows // CHUNKS), BF16),
                pltpu.VMEM((rows, head), F32),
                pltpu.VMEM((head, tokens), F32),
                pltpu.VMEM((head, tokens), F32),
                dma((6,)),
                dma((n_dev, CHUNKS)),
                dma((n_dev,)),
                dma((3, CHUNKS)),
                dma((3,)),
                dma((3, CHUNKS)),
                dma((3,)),
                dma((CHUNKS,)),
                dma((CHUNKS,)),
                dma,
            ],
            compiler_params=pltpu.CompilerParams(
                collective_id=0, has_side_effects=True),
            name='attention_backward',
        )(flat(q_tok), k_tok, v_tok, flat(fwd_out), flat(d_out), lse)
        return grad_q.reshape(tokens, groups, head), grad_k, grad_v

    return jax.shard_map(local_fn, mesh=mesh, in_specs=(row_spec,) * 6, out_specs=(row_spec,) * 3, check_vma=False)
```

time: 262 us -> 69 us (0.26); the launches traced: 258 us -> 68.8 us
  starting transfers between devices: 124 us -> 0 us
  waiting for transfers between devices: 88.9 us -> 0 us
  Pallas kernels: 0 us -> 62.4 us
  local copies, waits for them, and re-layouts: 25.5 us -> 5.8 us
  matrix products: 13 us -> 0 us
  other arithmetic: 5.87 us -> 0 us
    ppermute x30 -> x0, starting transfers between devices: 124 us -> none  [the longest x7 35.6 us: step_fn(): k_next = lax.ppermute(k_cur, 'cp', forward_perm)]
    ppermute x30 -> x0, waiting for transfers between devices: 88.9 us -> none  [the longest x7 21.6 us: step_fn(): dv_next = lax.ppermute(dv_acc, 'cp', forward_perm)]
    pallas_call x0 -> x1, Pallas kernels: none -> 62.4 us  [local_fn(): pl.pallas_call(functools.partial(kernel, rows, tokens, head), out_shape=(...]
    while x16 -> x0, local copies, waits for them, and re-layouts: 15.9 us -> none
    dot_general x5 -> x0, matrix products: 13 us -> none  [the longest x1 4.85 us: pair_update(): jnp.einsum('rgc,rgd->cd', prob_low, d_out, preferred_element_type=jnp.flo...]
    another operation x14 -> x0, local copies, waits for them, and re-layouts: 5.05 us -> none
    unnamed x2 -> x0, other arithmetic: 3.46 us -> none
  transfers between devices with their start and end apart: 30 -> 0, of which waited for: 23 -> 0; matrix products, arithmetic and copies ran while one was open for 6% -> 0% of each run, Pallas kernels for 0% -> 0%
where the time goes in v1:
time: 69 us; the launch traced here: 68.8 us
  Pallas kernels  62.4 us (90%)
  local copies, waits for them, and re-layouts  5.8 us (8%)
    pallas_call x1, Pallas kernels, local_fn(): pl.pallas_call(functools.partial(kernel, rows, tokens, head), out_shape=(...  62.4 us
    unnamed x8, local copies, waits for them, and re-layouts  4.9 us

profile of v1, /device:TPU:0, one launch (start us, length us, event | category | flops | bytes accessed | tf_op | source)
XLA Modules:
  0.0 68.8 jit_solution(12874030891380171555)
XLA Ops:
  0.6 0.9 %copy.10 = f32[1024,2]{1,0:T(8,128)S(1)} copy(f32[1024,2]{0,1:T(2,128)} %param.11) | data formatting | bytes 16384 | tf_op args[5]
  1.5 0.9 %reshape.24.lse_hbm = f32[4,4,128]{2,1,0:T(4,128)} reshape(f32[1024,2]{1,0:T(8,128)S(1)} %copy.10) | data formatting | bytes 16384 | tf_op jit(solution)/shard_map/reshape | solution.py:318
  2.4 62.4 %attention_backward.1 = (bf16[2048,128]{1,0:T(8,128)(2,1)}, bf16[1024,128]{1,0:T(8,128)(2,1)}, bf16[1024,128]{1,0:T(8,128)(2,1)}) custom-call(bf16[2048,128]{1,0:T(8,128)(2,1)} %bitcast.5, bf16[1024,128]{1,0:T(8,128)(2,1)} %k_hbm.1, bf16[1024,128]{1,0:T(8,128)(2,1)} %v_hbm.1, bf16[2048,128]{1,0:T(8,128)(2,1)} %bitcast.6, bf16[2048,128]{1,0:T(8,128)(2,1)} %bitcast.7, ...), custom_call_target="tpu_custom_call" | custom-call | tf_op jit(solution)/shard_map/attention_backward/pallas_call | solution.py:320
  64.8 0.0 copy-start.1
  64.9 2.2 %copy.14 = bf16[1024,2,128]{2,1,0:T(2,128)(2,1)} copy(bf16[1024,2,128]{2,1,0:T(2,128)(2,1)} %bitcast.4) | data formatting | bytes 1048576
  67.1 0.0 copy-done.1
  67.1 0.0 copy-start
  67.1 0.7 %copy.15 = bf16[1024,128]{1,0:T(8,128)(2,1)} copy(bf16[1024,128]{1,0:T(8,128)(2,1)S(1)} %copy-done.1) | data formatting | bytes 524288
  67.8 0.3 copy-done
  68.1 0.7 %copy.16 = bf16[1024,128]{1,0:T(8,128)(2,1)} copy(bf16[1024,128]{1,0:T(8,128)(2,1)S(1)} %copy-done) | data formatting | bytes 524288
Async XLA Ops:
  64.8 2.2 %copy-start.1 = (bf16[1024,128]{1,0:T(8,128)(2,1)S(1)}, bf16[1024,128]{1,0:T(8,128)(2,1)}, u32[]{:S(2)}) copy-start(bf16[1024,128]{1,0:T(8,128)(2,1)} %get-tuple-element.13) | copy-start | bytes 786436
  67.1 1.0 %copy-start = (bf16[1024,128]{1,0:T(8,128)(2,1)S(1)}, bf16[1024,128]{1,0:T(8,128)(2,1)}, u32[]{:S(2)}) copy-start(bf16[1024,128]{1,0:T(8,128)(2,1)} %get-tuple-element.14) | copy-start | bytes 786436

commit v2 on v1

v2 whole, which is shorter than its diff:
```python
import functools
import math

import jax
import jax.numpy as jnp
from jax import lax
from jax.experimental import pallas as pl
from jax.experimental.pallas import tpu as pltpu
from jax.sharding import PartitionSpec as P

BF16, F32 = jnp.bfloat16, jnp.float32
CHUNKS = 4
COLS = 256
STEPS = 14
MESH = pl.DeviceIdType.MESH


def dot(a, b):
    return jnp.dot(a, b, preferred_element_type=F32)


def beside(a, b):
    return jnp.concatenate([a, b], axis=1)


def parts(x):
    hi = x.astype(BF16).astype(F32)
    rest = x - hi
    md = rest.astype(BF16).astype(F32)
    return hi, md, rest - md


def kernel(rows, keys, head, n_dev, q_hbm, k_hbm, v_hbm, o_hbm, do_hbm, lse_hbm, dq_ref, dk_ref, dv_ref,
           qbuf, kvbuf, obuf, lse_in, auxr, own_aux, chunk_aux, k_one, v_one, own_qt, own_dot, own_kt, own_vt,
           q_t, do_t, dq_acc, dq_t, dk_t, dv_t,
           stage_sem, recv_sem, aux_recv, own_send, own_aux_send, pair_send, x_send, y_send):
    me = lax.axis_index('cp')
    core, px, py = me % 2, (me // 2) % 2, me // 4
    pair = me + 1 - 2 * core
    nx = me + 2 - 4 * px
    ny = me + 4 - 8 * py
    diag = nx + 4 - 8 * py
    other = pair - me
    mid = (px + py) == 1
    qc, kc = rows // CHUNKS, keys // CHUNKS
    scale = head ** -0.5
    exp_scale = scale * math.log2(math.e)

    def q_copy(slot, n, dest, send, recv):
        part = pl.ds(n * qc, qc)
        return pltpu.make_async_remote_copy(
            qbuf.at[slot, :, part], qbuf.at[slot, :, part], send, recv,
            device_id={'cp': dest}, device_id_type=MESH)

    def kv_copy(slot, n, dest, send, recv):
        part = pl.ds(n * kc, kc)
        return pltpu.make_async_remote_copy(
            kvbuf.at[slot, :, part], kvbuf.at[slot, :, part], send, recv,
            device_id={'cp': dest}, device_id_type=MESH)

    def aux_copy(slot, dest, send):
        return pltpu.make_async_remote_copy(
            auxr.at[slot], auxr.at[slot], send, aux_recv.at[slot],
            device_id={'cp': dest}, device_id_type=MESH)

    stages = [
        pltpu.make_async_copy(k_hbm, kvbuf.at[me, 0], stage_sem.at[0]),
        pltpu.make_async_copy(v_hbm, kvbuf.at[me, 1], stage_sem.at[1]),
        pltpu.make_async_copy(q_hbm, qbuf.at[me, 0], stage_sem.at[2]),
        pltpu.make_async_copy(do_hbm, qbuf.at[me, 1], stage_sem.at[3]),
        pltpu.make_async_copy(o_hbm, obuf, stage_sem.at[4]),
        pltpu.make_async_copy(lse_hbm, lse_in, stage_sem.at[5]),
    ]
    for s in stages:
        s.start()

    barrier = pltpu.get_barrier_semaphore()
    for peer in range(n_dev):
        @pl.when(peer != me)
        def _():
            pl.semaphore_signal(barrier, inc=1, device_id={'cp': peer}, device_id_type=MESH)
    pl.semaphore_wait(barrier, n_dev - 1)

    def order(d, n):
        return (n + 2) % CHUNKS if d == 1 else n

    dests = (pair, nx, ny)
    for s in stages[:4]:
        s.wait()
    for d, dest in enumerate(dests):
        @pl.when(dest > me)
        def _():
            for n in range(CHUNKS):
                c = order(d, n)
                kv_copy(me, c, dest, own_send.at[d, c], recv_sem.at[me, c]).start()

        @pl.when(dest < me)
        def _():
            c = order(d, 0)
            q_copy(me, c, dest, own_send.at[d, c], recv_sem.at[me, c]).start()

    for s in stages[4:]:
        s.wait()

    at_row = lax.broadcasted_iota(jnp.int32, (COLS, COLS), 0)
    at_col = lax.broadcasted_iota(jnp.int32, (COLS, COLS), 1)
    weave = jnp.where(at_col == 2 * (at_row % 128) + at_row // 128, 1.0, 0.0).astype(BF16)
    sub = lax.broadcasted_iota(jnp.int32, (16, 128), 0)
    for g in range(rows // 256):
        sides = []
        for h in range(2):
            row = lse_in[h:h + 1, g * 128:(g + 1) * 128] * (1.0 / scale)
            hi, md, lo = parts(row)
            sides.append(jnp.where(sub == 0, hi, jnp.where(sub == 1, md, jnp.where(sub == 2, lo, 0.0))))
        woven = dot(beside(*sides).astype(BF16), weave)
        row = woven[0:1] + (woven[1:2] + woven[2:3])
        n, at = g // 2, (g % 2) * 2
        auxr[me, n, at:at + 1] = row[:, 0:128]
        auxr[me, n, at + 1:at + 2] = row[:, 128:256]

    def delta_rows(n, _):
        for g in range(qc // 128):
            part = pl.ds(pl.multiple_of(n * qc + g * 128, 128), 128)
            d = jnp.sum(qbuf[me, 1, part].astype(F32) * obuf[part].astype(F32), axis=1, keepdims=True)
            auxr[me, n, 4 + g:5 + g] = jnp.transpose(jnp.broadcast_to(d, (128, 128)))[0:1]
        return 0

    lax.fori_loop(0, CHUNKS, delta_rows, 0)

    def aux_lines(slot, n):
        hi, md, lo = parts(auxr[slot, n])
        sub = lax.broadcasted_iota(jnp.int32, (8, 128), 0)
        lines = []
        for g in range(qc // 128):
            m = jnp.zeros((8, 128), F32)
            for i, row in enumerate((hi[g:g + 1], md[g:g + 1], lo[g:g + 1],
                                     hi[4 + g:5 + g], md[4 + g:5 + g], lo[4 + g:5 + g])):
                m = jnp.where(sub == i, row, m)
            lines.append(jnp.concatenate([m, jnp.zeros((120, 128), F32)], axis=0))
        return lines

    def fill_aux(slot, n, dst, base):
        for g, m in enumerate(aux_lines(slot, n)):
            dst[pl.ds(base + g * 128, 128)] = jnp.transpose(m).astype(BF16)

    lane = lax.broadcasted_iota(jnp.int32, (COLS, head), 1)
    line = lax.broadcasted_iota(jnp.int32, (head, keys), 0)
    k_one[...] = jnp.where(lane < 3, -1.0, 0.0).astype(BF16)
    v_one[...] = jnp.where((lane >= 3) & (lane < 6), -1.0, 0.0).astype(BF16)
    own_kt[head:] = jnp.where(line < 3, -1.0, 0.0).astype(BF16)
    own_vt[head:] = jnp.where((line >= 3) & (line < 6), -1.0, 0.0).astype(BF16)
    dk_t[...] = jnp.zeros_like(dk_t)
    dv_t[...] = jnp.zeros_like(dv_t)
    dq_t[...] = jnp.zeros_like(dq_t)

    def own_fill(n, _):
        base = pl.multiple_of(n * qc, 128)
        part, kpart = pl.ds(base, qc), pl.ds(pl.multiple_of(n * kc, 128), kc)
        for g, m in enumerate(aux_lines(me, n)):
            at = pl.ds(pl.multiple_of(base + g * 128, 128), 128)
            own_aux[at] = jnp.transpose(m).astype(BF16)
            own_qt[head:, at] = m.astype(BF16)
            own_dot[head:, at] = m.astype(BF16)
        own_qt[:head, part] = jnp.transpose(qbuf[me, 0, part])
        own_dot[:head, part] = jnp.transpose(qbuf[me, 1, part])
        own_kt[:head, kpart] = jnp.transpose(kvbuf[me, 0, kpart])
        own_vt[:head, kpart] = jnp.transpose(kvbuf[me, 1, kpart])
        return 0

    lax.fori_loop(0, CHUNKS, own_fill, 0)

    for rb in range(CHUNKS):
        rpart = pl.ds(rb * qc, qc)
        aux = own_aux[rpart]
        q, do = beside(qbuf[me, 0, rpart], aux), beside(qbuf[me, 1, rpart], aux)
        dq = None
        for cb in range(rb + 1):
            cpart = pl.ds(cb * kc, kc)
            p = jnp.exp2(dot(q, own_kt[:, cpart]) * exp_scale)
            d = dot(do, own_vt[:, cpart])
            if cb == rb:
                row = lax.broadcasted_iota(jnp.int32, (qc, kc), 0)
                col = lax.broadcasted_iota(jnp.int32, (qc, kc), 1)
                p = jnp.where(2 * col <= row, p, 0.0)
            ds = (p * d).astype(BF16)
            dv_t[:, cpart] += dot(own_dot[:head, rpart], p.astype(BF16))
            dk_t[:, cpart] += dot(own_qt[:head, rpart], ds)
            term = dot(ds, kvbuf[me, 0, cpart])
            dq = term if dq is None else dq + term
        dq_acc[rpart] = dq

    for peer in range(n_dev):
        @pl.when(peer < me)
        def _():
            aux_copy(me, peer, own_aux_send.at[peer]).start()
    for d, dest in enumerate(dests):
        @pl.when(dest < me)
        def _():
            for n in range(1, CHUNKS):
                c = order(d, n)
                q_copy(me, c, dest, own_send.at[d, c], recv_sem.at[me, c]).start()

    def plan(t):
        na, ka = (t - 2) // 2, t % 2
        nb = (t - 10) // 2
        first, second = t < 2, t < 10
        hop = jnp.where(ka == 1, other, 0)

        def pick(a, b, c):
            return jnp.where(first, a, jnp.where(second, b, c))

        stream_a = pick(3, jnp.where(ka == 0, 0, 3), jnp.where(ka == 0, 2, 3))
        stream_b = pick(3, jnp.where(ka == 0, 1, 3), jnp.where(ka == 0, 2, 3))
        src_a = pick(pair, nx + hop, diag + hop)
        src_b = pick(pair, ny + hop, diag + hop)
        piece_a = pick(2 * t, (na + 2) % CHUNKS, jnp.where(mid, 2 * nb, nb))
        piece_b = pick(2 * t + 1, na, jnp.where(mid, 2 * nb + 1, nb + 2))
        swap = (src_a > me) & (src_b < me)

        def swapped(a, b):
            return jnp.where(swap, b, a), jnp.where(swap, a, b)

        stream_a, stream_b = swapped(stream_a, stream_b)
        src_a, src_b = swapped(src_a, src_b)
        piece_a, piece_b = swapped(piece_a, piece_b)
        return (stream_a, src_a, piece_a), (stream_b, src_b, piece_b)

    def sends(item, do):
        stream, src, piece = item
        idx = jnp.minimum(stream, 2)
        recv = recv_sem.at[src, piece]
        to_x = (stream == 1) & (jnp.logical_not(mid) | (piece < 2))
        to_y = (stream == 0) & mid & (piece >= 2)
        for make, want in ((q_copy, src > me), (kv_copy, src < me)):
            @pl.when(want)
            def _():
                do(make(src, piece, me, x_send.at[piece], recv), 'recv')

                @pl.when(to_x)
                def _():
                    do(make(src, piece, nx, x_send.at[piece], recv), 'send')

                @pl.when(to_y)
                def _():
                    do(make(src, piece, ny, y_send.at[piece], recv), 'send')

                @pl.when(stream < 3)
                def _():
                    do(make(src, piece, pair, pair_send.at[idx, piece], recv), 'send')

    def arrive(copy, what):
        copy.wait_recv() if what == 'recv' else copy.start()

    def leave(copy, what):
        if what == 'send':
            copy.wait_send()

    def add_keys_grads(items, cur):
        loaded = []
        for idx, (_, src, piece) in items:
            part = pl.ds(pl.multiple_of(piece * qc, qc), qc)
            q, do, aux = qbuf[src, 0, part], qbuf[src, 1, part], chunk_aux[cur, idx]
            q_t[idx] = jnp.transpose(q)
            do_t[idx] = jnp.transpose(do)
            loaded.append((idx, beside(q, aux), beside(do, aux)))
        for cb in range(keys // COLS):
            cpart = pl.ds(cb * COLS, COLS)
            dv = dk = None
            for idx, q, do in loaded:
                p = jnp.exp2(dot(q, own_kt[:, cpart]) * exp_scale)
                ds = (p * dot(do, own_vt[:, cpart])).astype(BF16)
                tv, tk = dot(do_t[idx], p.astype(BF16)), dot(q_t[idx], ds)
                dv, dk = (tv, tk) if dv is None else (dv + tv, dk + tk)
            dv_t[:, cpart] += dv
            dk_t[:, cpart] += dk

    def add_rows_grad(items):
        ks, vs = [], []
        for idx, (_, src, piece) in items:
            part = pl.ds(pl.multiple_of(piece * kc, kc), kc)
            ks.append(kvbuf[src, 0, part])
            vs.append(kvbuf[src, 1, part])
        k_ts = [jnp.transpose(k) for k in ks]
        k = jnp.concatenate([beside(k, k_one[...]) for k in ks], axis=0)
        v = jnp.concatenate([beside(v, v_one[...]) for v in vs], axis=0)
        k_t = k_ts[0] if len(k_ts) == 1 else beside(*k_ts)
        for rb in range(rows // COLS):
            part = pl.ds(rb * COLS, COLS)
            p = jnp.exp2(dot(k, own_qt[:, part]) * exp_scale)
            ds = (p * dot(v, own_dot[:, part])).astype(BF16)
            dq_t[:, part] += dot(k_t, ds)

    def prefetch(t, idx):
        _, src, piece = plan(t)[idx]
        fill_aux(jnp.where(src > me, src, me), piece, chunk_aux.at[t % 2, idx], 0)

    @pl.when(pair > me)
    def _():
        aux_copy(pair, me, own_aux_send.at[0]).wait_recv()
        for idx in range(2):
            prefetch(0, idx)

    def step(t, _):
        a, b = plan(t)
        cur = t % 2

        @pl.when(t == 1)
        def _():
            for peer in range(n_dev):
                @pl.when((peer > me) & (peer != pair))
                def _():
                    aux_copy(peer, me, own_aux_send.at[0]).wait_recv()

        sends(a, arrive)
        sends(b, arrive)
        a_keys, b_keys = a[1] < me, b[1] < me
        later = jnp.minimum(t + 1, STEPS - 1)

        def ahead():
            for idx in range(2):
                _, src, piece = plan(later)[idx]
                fill_aux(jnp.where(src > me, src, me), piece, chunk_aux.at[1 - cur, idx], 0)

        @pl.when(jnp.logical_not(a_keys))
        def _():
            add_keys_grads(((0, a), (1, b)), cur)
            ahead()

        @pl.when(a_keys & b_keys)
        def _():
            add_rows_grad(((0, a), (1, b)))
            ahead()

        @pl.when(a_keys & jnp.logical_not(b_keys))
        def _():
            add_rows_grad(((0, a),))
            add_keys_grads(((1, b),), cur)
            ahead()

        return 0

    lax.fori_loop(0, STEPS, step, 0)

    dq_ref[...] = ((dq_acc[...] + jnp.transpose(dq_t[...])) * scale).astype(BF16)
    dk_ref[...] = (jnp.transpose(dk_t[...]) * scale).astype(BF16)
    dv_ref[...] = jnp.transpose(dv_t[...]).astype(BF16)

    for peer in range(n_dev):
        @pl.when(peer < me)
        def _():
            aux_copy(me, peer, own_aux_send.at[peer]).wait_send()
    for d, dest in enumerate(dests):
        for make, want in ((kv_copy, dest > me), (q_copy, dest < me)):
            @pl.when(want)
            def _():
                for c in range(CHUNKS):
                    make(me, c, dest, own_send.at[d, c], recv_sem.at[me, c]).wait_send()

    def drain(t, _):
        for item in plan(t):
            sends(item, leave)
        return 0

    lax.fori_loop(2, STEPS, drain, 0)


def solution(mesh):
    n_dev = mesh.shape['cp']
    row_spec = P(('dp', 'cp'))

    def local_fn(q_tok, k_tok, v_tok, fwd_out, d_out, lse_row):
        tokens, groups, head = q_tok.shape
        rows = tokens * groups
        piece = rows // CHUNKS
        flat = lambda x: x.reshape(rows, head)
        dma = pltpu.SemaphoreType.DMA
        vmem = pltpu.VMEM
        grad_q, grad_k, grad_v = pl.pallas_call(
            functools.partial(kernel, rows, tokens, head, n_dev),
            out_shape=(jax.ShapeDtypeStruct((rows, head), BF16),
                       jax.ShapeDtypeStruct((tokens, head), BF16),
                       jax.ShapeDtypeStruct((tokens, head), BF16)),
            in_specs=[pl.BlockSpec(memory_space=pltpu.HBM)] * 6,
            out_specs=(pl.BlockSpec(memory_space=vmem),) * 3,
            scratch_shapes=[
                vmem((n_dev, 2, rows, head), BF16),
                vmem((n_dev, 2, tokens, head), BF16),
                vmem((rows, head), BF16),
                vmem((groups, tokens), F32),
                vmem((n_dev, CHUNKS, 8, 128), F32),
                vmem((rows, head), BF16),
                vmem((2, 2, piece, head), BF16),
                vmem((COLS, head), BF16),
                vmem((COLS, head), BF16),
                vmem((2 * head, rows), BF16),
                vmem((2 * head, rows), BF16),
                vmem((2 * head, tokens), BF16),
                vmem((2 * head, tokens), BF16),
                vmem((2, head, piece), BF16),
                vmem((2, head, piece), BF16),
                vmem((rows, head), F32),
                vmem((head, rows), F32),
                vmem((head, tokens), F32),
                vmem((head, tokens), F32),
                dma((6,)),
                dma((n_dev, CHUNKS)),
                dma((n_dev,)),
                dma((3, CHUNKS)),
                dma((n_dev,)),
                dma((3, CHUNKS)),
                dma((CHUNKS,)),
                dma((CHUNKS,)),
            ],
            compiler_params=pltpu.CompilerParams(
                collective_id=0, has_side_effects=True, vmem_limit_bytes=48 * 1024 * 1024),
            name='attention_backward',
        )(flat(q_tok), k_tok, v_tok, flat(fwd_out), flat(d_out), lse_row.T)
        return grad_q.reshape(tokens, groups, head), grad_k, grad_v

    return jax.shard_map(local_fn, mesh=mesh, in_specs=(row_spec,) * 6, out_specs=(row_spec,) * 3, check_vma=False)
```

time: 69 us -> 65.5 us (0.949)
  the two profiles are of different devices: /device:TPU:0 before, /device:TPU:3 now
where the time goes in v2:
time: 65.5 us; the launch traced here: 65.1 us
  Pallas kernels  56.6 us (86%)
  local copies, waits for them, and re-layouts  7.91 us (12%)
  between operations  0.66 us (1%)
    pallas_call x1, Pallas kernels, local_fn(): pl.pallas_call(functools.partial(kernel, rows, tokens, head, n_dev), out_...  56.6 us
    unnamed x15, local copies, waits for them, and re-layouts  7.91 us

profile of v2, /device:TPU:3, one launch (start us, length us, event | category | flops | bytes accessed | tf_op | source)
XLA Modules:
  0.0 65.1 jit_solution(12738935800986443077)
XLA Ops:
  0.6 0.0 copy-start
  0.6 1.0 %copy-done = bf16[1024,2,128]{2,1,0:T(2,128)(2,1)S(1)} copy-done((bf16[1024,2,128]{2,1,0:T(2,128)(2,1)S(1)}, bf16[1024,2,128]{2,1,0:T(2,128)(2,1)}, u32[]{:S(2)}) %copy-start) | copy-done | bytes 524312
  1.7 0.0 copy-start.1
  1.7 1.0 %copy-done.1 = bf16[1024,2,128]{2,1,0:T(2,128)(2,1)S(1)} copy-done((bf16[1024,2,128]{2,1,0:T(2,128)(2,1)S(1)}, bf16[1024,2,128]{2,1,0:T(2,128)(2,1)}, u32[]{:S(2)}) %copy-start.1) | copy-done | bytes 524312
  2.7 0.0 copy-start.2
  2.7 1.0 %copy-done.2 = bf16[1024,2,128]{2,1,0:T(2,128)(2,1)S(1)} copy-done((bf16[1024,2,128]{2,1,0:T(2,128)(2,1)S(1)}, bf16[1024,2,128]{2,1,0:T(2,128)(2,1)}, u32[]{:S(2)}) %copy-start.2) | copy-done | bytes 524312
  3.8 0.0 copy-start.3
  3.8 0.9 %copy-done.3 = bf16[1024,128]{1,0:T(8,128)(2,1)S(1)} copy-done((bf16[1024,128]{1,0:T(8,128)(2,1)S(1)}, bf16[1024,128]{1,0:T(8,128)(2,1)}, u32[]{:S(2)}) %copy-start.3) | copy-done | bytes 262168
  4.7 0.0 copy-start.4
  4.7 0.9 %copy-done.4 = bf16[1024,128]{1,0:T(8,128)(2,1)S(1)} copy-done((bf16[1024,128]{1,0:T(8,128)(2,1)S(1)}, bf16[1024,128]{1,0:T(8,128)(2,1)}, u32[]{:S(2)}) %copy-start.4) | copy-done | bytes 262168
  5.7 0.0 copy-start.5
  5.7 0.7 %copy-done.5 = f32[1024,2]{0,1:T(2,128)S(1)} copy-done((f32[1024,2]{0,1:T(2,128)S(1)}, f32[1024,2]{0,1:T(2,128)}, u32[]{:S(2)}) %copy-start.5) | copy-done | bytes 8216
  6.4 56.6 %attention_backward.1 = (bf16[2048,128]{1,0:T(8,128)(2,1)S(1)}, bf16[1024,128]{1,0:T(8,128)(2,1)S(1)}, bf16[1024,128]{1,0:T(8,128)(2,1)S(1)}) custom-call(bf16[2048,128]{1,0:T(8,128)(2,1)S(1)} %bitcast.6, bf16[1024,128]{1,0:T(8,128)(2,1)S(1)} %copy-done.3, bf16[1024,128]{1,0:T(8,128)(2,1)S(1)} %copy-done.4, bf16[2048,128]{1,0:T(8,128)(2,1)S(1)} %bitcast.7, ...), custom_call_target="tpu_custom_call" | custom-call | tf_op jit(solution)/shard_map/attention_backward/pallas_call | solution.py:378
  62.9 0.8 %copy.12 = bf16[1024,2,128]{2,1,0:T(2,128)(2,1)} copy(bf16[1024,2,128]{2,1,0:T(2,128)(2,1)S(1)} %bitcast.5) | data formatting | bytes 1048576
  63.7 0.7 %copy.13 = bf16[1024,128]{1,0:T(8,128)(2,1)} copy(bf16[1024,128]{1,0:T(8,128)(2,1)S(1)} %get-tuple-element.13) | data formatting | bytes 524288
  64.4 0.7 %copy.14 = bf16[1024,128]{1,0:T(8,128)(2,1)} copy(bf16[1024,128]{1,0:T(8,128)(2,1)S(1)} %get-tuple-element.14) | data formatting | bytes 524288
Async XLA Ops:
  0.6 1.0 %copy-start = (bf16[1024,2,128]{2,1,0:T(2,128)(2,1)S(1)}, bf16[1024,2,128]{2,1,0:T(2,128)(2,1)}, u32[]{:S(2)}) copy-start(bf16[1024,2,128]{2,1,0:T(2,128)(2,1)} %param.6) | copy-start | bytes 1572868
  1.7 1.0 %copy-start.1 = (bf16[1024,2,128]{2,1,0:T(2,128)(2,1)S(1)}, bf16[1024,2,128]{2,1,0:T(2,128)(2,1)}, u32[]{:S(2)}) copy-start(bf16[1024,2,128]{2,1,0:T(2,128)(2,1)} %param.9) | copy-start | bytes 1572868
  2.7 1.0 %copy-start.2 = (bf16[1024,2,128]{2,1,0:T(2,128)(2,1)S(1)}, bf16[1024,2,128]{2,1,0:T(2,128)(2,1)}, u32[]{:S(2)}) copy-start(bf16[1024,2,128]{2,1,0:T(2,128)(2,1)} %param.10) | copy-start | bytes 1572868
  3.8 0.9 %copy-start.3 = (bf16[1024,128]{1,0:T(8,128)(2,1)S(1)}, bf16[1024,128]{1,0:T(8,128)(2,1)}, u32[]{:S(2)}) copy-start(bf16[1024,128]{1,0:T(8,128)(2,1)} %k_hbm.1) | copy-start | bytes 786436
  4.7 0.9 %copy-start.4 = (bf16[1024,128]{1,0:T(8,128)(2,1)S(1)}, bf16[1024,128]{1,0:T(8,128)(2,1)}, u32[]{:S(2)}) copy-start(bf16[1024,128]{1,0:T(8,128)(2,1)} %v_hbm.1) | copy-start | bytes 786436
  5.7 0.7 %copy-start.5 = (f32[1024,2]{0,1:T(2,128)S(1)}, f32[1024,2]{0,1:T(2,128)}, u32[]{:S(2)}) copy-start(f32[1024,2]{0,1:T(2,128)} %param.11) | copy-start | bytes 24580

commit v3 on v2

--- a/solution.py
+++ b/solution.py
@@ -284,8 +284,8 @@
         k = jnp.concatenate([beside(k, k_one[...]) for k in ks], axis=0)
         v = jnp.concatenate([beside(v, v_one[...]) for v in vs], axis=0)
         k_t = k_ts[0] if len(k_ts) == 1 else beside(*k_ts)
-        for rb in range(rows // COLS):
-            part = pl.ds(rb * COLS, COLS)
+        for rb in range(rows // 512):
+            part = pl.ds(rb * 512, 512)
             p = jnp.exp2(dot(k, own_qt[:, part]) * exp_scale)
             ds = (p * dot(v, own_dot[:, part])).astype(BF16)
             dq_t[:, part] += dot(k_t, ds)
@@ -362,6 +362,15 @@
         return 0
 
     lax.fori_loop(2, STEPS, drain, 0)
+
+
+def store(*refs):
+    n = len(refs) // 2
+    copies = [pltpu.make_async_copy(refs[i], refs[n + i], refs[-1].at[i]) for i in range(n)]
+    for c in copies:
+        c.start()
+    for c in copies:
+        c.wait()
 
 
 def solution(mesh):
@@ -414,7 +423,18 @@
             compiler_params=pltpu.CompilerParams(
                 collective_id=0, has_side_effects=True, vmem_limit_bytes=48 * 1024 * 1024),
             name='attention_backward',
-        )(flat(q_tok), k_tok, v_tok, flat(fwd_out), flat(d_out), lse_row.T)
+        )(*[pltpu.with_memory_space_constraint(x, pltpu.HBM) for x in (flat(q_tok), k_tok, v_tok, flat(fwd_out), flat(d_out), lse_row.T)])
+        grads = (grad_q, grad_k, grad_v)
+        any_space = pl.BlockSpec(memory_space=pl.ANY)
+        grad_q, grad_k, grad_v = pl.pallas_call(
+            store,
+            out_shape=tuple(jax.ShapeDtypeStruct(g.shape, g.dtype) for g in grads),
+            in_specs=[any_space] * 3,
+            out_specs=(any_space,) * 3,
+            scratch_shapes=[dma((3,))],
+            compiler_params=pltpu.CompilerParams(vmem_limit_bytes=1024 * 1024),
+            name='store_grads',
+        )(*[pltpu.with_memory_space_constraint(g, vmem) for g in grads])
         return grad_q.reshape(tokens, groups, head), grad_k, grad_v
 
     return jax.shard_map(local_fn, mesh=mesh, in_specs=(row_spec,) * 6, out_specs=(row_spec,) * 3, check_vma=False)

time: 65.5 us -> 54.6 us (0.83)
  the two profiles are of different devices: /device:TPU:3 before, /device:TPU:2 now
where the time goes in v3:
time: 54.6 us; the launch traced here: 54.5 us
  Pallas kernels  53.8 us (99%)
  between operations  0.64 us (1%)
    pallas_call x1, Pallas kernels, local_fn(): pl.pallas_call(functools.partial(kernel, rows, tokens, head, n_dev), out_...  52.9 us

profile of v3, /device:TPU:2, one launch (start us, length us, event | category | flops | bytes accessed | tf_op | source)
XLA Modules:
  0.0 54.5 jit_solution(11357682450487005170)
XLA Ops:
  0.6 52.9 %attention_backward.1 = (bf16[2048,128]{1,0:T(8,128)(2,1)S(1)}, bf16[1024,128]{1,0:T(8,128)(2,1)S(1)}, bf16[1024,128]{1,0:T(8,128)(2,1)S(1)}) custom-call(bf16[2048,128]{1,0:T(8,128)(2,1)} %bitcast.5, bf16[1024,128]{1,0:T(8,128)(2,1)} %k_hbm.1, bf16[1024,128]{1,0:T(8,128)(2,1)} %v_hbm.1, bf16[2048,128]{1,0:T(8,128)(2,1)} %bitcast.6, ...), custom_call_target="tpu_custom_call" | custom-call | tf_op jit(solution)/shard_map/attention_backward/pallas_call | solution.py:387
  53.5 1.0 %store_grads.1 = (bf16[2048,128]{1,0:T(8,128)(2,1)}, bf16[1024,128]{1,0:T(8,128)(2,1)}, bf16[1024,128]{1,0:T(8,128)(2,1)}) custom-call(bf16[2048,128]{1,0:T(8,128)(2,1)S(1)} %get-tuple-element.9.refs_0_, bf16[1024,128]{1,0:T(8,128)(2,1)S(1)} %get-tuple-element.10.refs_1_, bf16[1024,128]{1,0:T(8,128)(2,1)S(1)} %get-tuple-element.11.refs_2_), custom_call_target="tpu_custom_call" | custom-call | tf_op jit(solution)/shard_map/store_grads/pallas_call | solution.py:429

commit v4 on v3

--- a/solution.py
+++ b/solution.py
@@ -92,12 +92,12 @@
         def _():
             for n in range(CHUNKS):
                 c = order(d, n)
-                kv_copy(me, c, dest, own_send.at[d, c], recv_sem.at[me, c]).start()
+                kv_copy(me, c, dest, own_send.at[d], recv_sem.at[me, c]).start()
 
         @pl.when(dest < me)
         def _():
             c = order(d, 0)
-            q_copy(me, c, dest, own_send.at[d, c], recv_sem.at[me, c]).start()
+            q_copy(me, c, dest, own_send.at[d], recv_sem.at[me, c]).start()
 
     for s in stages[4:]:
         s.wait()
@@ -168,6 +168,17 @@
         return 0
 
     lax.fori_loop(0, CHUNKS, own_fill, 0)
+
+    for peer in range(n_dev):
+        @pl.when(peer < me)
+        def _():
+            aux_copy(me, peer, own_aux_send.at[peer]).start()
+    for d, dest in enumerate(dests):
+        @pl.when(dest < me)
+        def _():
+            for n in range(1, CHUNKS):
+                c = order(d, n)
+                q_copy(me, c, dest, own_send.at[d], recv_sem.at[me, c]).start()
 
     for rb in range(CHUNKS):
         rpart = pl.ds(rb * qc, qc)
@@ -189,17 +200,6 @@
             dq = term if dq is None else dq + term
         dq_acc[rpart] = dq
 
-    for peer in range(n_dev):
-        @pl.when(peer < me)
-        def _():
-            aux_copy(me, peer, own_aux_send.at[peer]).start()
-    for d, dest in enumerate(dests):
-        @pl.when(dest < me)
-        def _():
-            for n in range(1, CHUNKS):
-                c = order(d, n)
-                q_copy(me, c, dest, own_send.at[d, c], recv_sem.at[me, c]).start()
-
     def plan(t):
         na, ka = (t - 2) // 2, t % 2
         nb = (t - 10) // 2
@@ -225,7 +225,7 @@
         piece_a, piece_b = swapped(piece_a, piece_b)
         return (stream_a, src_a, piece_a), (stream_b, src_b, piece_b)
 
-    def sends(item, do):
+    def arrive(item):
         stream, src, piece = item
         idx = jnp.minimum(stream, 2)
         recv = recv_sem.at[src, piece]
@@ -234,26 +234,19 @@
         for make, want in ((q_copy, src > me), (kv_copy, src < me)):
             @pl.when(want)
             def _():
-                do(make(src, piece, me, x_send.at[piece], recv), 'recv')
+                make(src, piece, me, x_send, recv).wait_recv()
 
                 @pl.when(to_x)
                 def _():
-                    do(make(src, piece, nx, x_send.at[piece], recv), 'send')
+                    make(src, piece, nx, x_send, recv).start()
 
                 @pl.when(to_y)
                 def _():
-                    do(make(src, piece, ny, y_send.at[piece], recv), 'send')
+                    make(src, piece, ny, y_send, recv).start()
 
                 @pl.when(stream < 3)
                 def _():
-                    do(make(src, piece, pair, pair_send.at[idx, piece], recv), 'send')
-
-    def arrive(copy, what):
-        copy.wait_recv() if what == 'recv' else copy.start()
-
-    def leave(copy, what):
-        if what == 'send':
-            copy.wait_send()
+                    make(src, piece, pair, pair_send.at[idx], recv).start()
 
     def add_keys_grads(items, cur):
         loaded = []
@@ -311,8 +304,8 @@
                 def _():
                     aux_copy(peer, me, own_aux_send.at[0]).wait_recv()
 
-        sends(a, arrive)
-        sends(b, arrive)
+        arrive(a)
+        arrive(b)
         a_keys, b_keys = a[1] < me, b[1] < me
         later = jnp.minimum(t + 1, STEPS - 1)
 
@@ -349,19 +342,22 @@
         @pl.when(peer < me)
         def _():
             aux_copy(me, peer, own_aux_send.at[peer]).wait_send()
-    for d, dest in enumerate(dests):
-        for make, want in ((kv_copy, dest > me), (q_copy, dest < me)):
-            @pl.when(want)
-            def _():
-                for c in range(CHUNKS):
-                    make(me, c, dest, own_send.at[d, c], recv_sem.at[me, c]).wait_send()
-
-    def drain(t, _):
-        for item in plan(t):
-            sends(item, leave)
-        return 0
-
-    lax.fori_loop(2, STEPS, drain, 0)
+
+    def left(buf, slot, length, send, want):
+        @pl.when(want)
+        def _():
+            block = buf.at[slot, :, pl.ds(0, length)]
+            pltpu.make_async_remote_copy(block, block, send, recv_sem.at[slot, 0],
+                                         device_id={'cp': pair}, device_id_type=MESH).wait_send()
+
+    for buf, size, sign in ((qbuf, rows, 1), (kvbuf, keys, -1)):
+        for d, dest in enumerate(dests):
+            left(buf, me, size, own_send.at[d], sign * dest < sign * me)
+        for d, src in enumerate((nx, ny, diag)):
+            left(buf, src, size, pair_send.at[d], sign * src > sign * me)
+        left(buf, ny, size, x_send, (sign * ny > sign * me) & jnp.logical_not(mid))
+        left(buf, ny, size // 2, x_send, (sign * ny > sign * me) & mid)
+        left(buf, nx, size // 2, y_send, (sign * nx > sign * me) & mid)
 
 
 def store(*refs):
@@ -414,11 +410,11 @@
                 dma((6,)),
                 dma((n_dev, CHUNKS)),
                 dma((n_dev,)),
-                dma((3, CHUNKS)),
+                dma((3,)),
                 dma((n_dev,)),
-                dma((3, CHUNKS)),
-                dma((CHUNKS,)),
-                dma((CHUNKS,)),
+                dma((3,)),
+                dma,
+                dma,
             ],
             compiler_params=pltpu.CompilerParams(
                 collective_id=0, has_side_effects=True, vmem_limit_bytes=48 * 1024 * 1024),

time: 54.6 us -> 53.7 us (0.984)
  Pallas kernels: 53.8 us -> 52.9 us
    pallas_call x1, Pallas kernels: 52.9 us -> 51.9 us  [local_fn(): pl.pallas_call(functools.partial(kernel, rows, tokens, head, n_dev), out_...]
where the time goes in v4:
time: 53.7 us; the launch traced here: 53.6 us
  Pallas kernels  52.9 us (99%)
  between operations  0.64 us (1%)
    pallas_call x1, Pallas kernels, local_fn(): pl.pallas_call(functools.partial(kernel, rows, tokens, head, n_dev), out_...  51.9 us

profile of v4, /device:TPU:2, one launch (start us, length us, event | category | flops | bytes accessed | tf_op | source)
XLA Modules:
  0.0 53.6 jit_solution(16545379378825308410)
XLA Ops:
  0.6 51.9 %attention_backward.1 = (bf16[2048,128]{1,0:T(8,128)(2,1)S(1)}, bf16[1024,128]{1,0:T(8,128)(2,1)S(1)}, bf16[1024,128]{1,0:T(8,128)(2,1)S(1)}) custom-call(bf16[2048,128]{1,0:T(8,128)(2,1)} %bitcast.5, bf16[1024,128]{1,0:T(8,128)(2,1)} %k_hbm.1, bf16[1024,128]{1,0:T(8,128)(2,1)} %v_hbm.1, bf16[2048,128]{1,0:T(8,128)(2,1)} %bitcast.6, ...), custom_call_target="tpu_custom_call" | custom-call | tf_op jit(solution)/shard_map/attention_backward/pallas_call | solution.py:383
  52.6 1.0 %store_grads.1 = (bf16[2048,128]{1,0:T(8,128)(2,1)}, bf16[1024,128]{1,0:T(8,128)(2,1)}, bf16[1024,128]{1,0:T(8,128)(2,1)}) custom-call(bf16[2048,128]{1,0:T(8,128)(2,1)S(1)} %get-tuple-element.9.refs_0_, bf16[1024,128]{1,0:T(8,128)(2,1)S(1)} %get-tuple-element.10.refs_1_, bf16[1024,128]{1,0:T(8,128)(2,1)S(1)} %get-tuple-element.11.refs_2_), custom_call_target="tpu_custom_call" | custom-call | tf_op jit(solution)/shard_map/store_grads/pallas_call | solution.py:425

commit v5 on v4

--- a/solution.py
+++ b/solution.py
@@ -12,6 +12,9 @@
 CHUNKS = 4
 COLS = 256
 STEPS = 14
+LEAD_Q, LEAD_K, LEAD_M = 4, 4, 2
+LEAD_D = 2
+WIDTH_K, WIDTH_M = 256, 512
 MESH = pl.DeviceIdType.MESH
 
 
@@ -149,8 +152,6 @@
     v_one[...] = jnp.where((lane >= 3) & (lane < 6), -1.0, 0.0).astype(BF16)
     own_kt[head:] = jnp.where(line < 3, -1.0, 0.0).astype(BF16)
     own_vt[head:] = jnp.where((line >= 3) & (line < 6), -1.0, 0.0).astype(BF16)
-    dk_t[...] = jnp.zeros_like(dk_t)
-    dv_t[...] = jnp.zeros_like(dv_t)
     dq_t[...] = jnp.zeros_like(dq_t)
 
     def own_fill(n, _):
@@ -180,25 +181,50 @@
                 c = order(d, n)
                 q_copy(me, c, dest, own_send.at[d], recv_sem.at[me, c]).start()
 
-    for rb in range(CHUNKS):
-        rpart = pl.ds(rb * qc, qc)
-        aux = own_aux[rpart]
-        q, do = beside(qbuf[me, 0, rpart], aux), beside(qbuf[me, 1, rpart], aux)
-        dq = None
-        for cb in range(rb + 1):
-            cpart = pl.ds(cb * kc, kc)
-            p = jnp.exp2(dot(q, own_kt[:, cpart]) * exp_scale)
-            d = dot(do, own_vt[:, cpart])
-            if cb == rb:
-                row = lax.broadcasted_iota(jnp.int32, (qc, kc), 0)
-                col = lax.broadcasted_iota(jnp.int32, (qc, kc), 1)
-                p = jnp.where(2 * col <= row, p, 0.0)
-            ds = (p * d).astype(BF16)
-            dv_t[:, cpart] += dot(own_dot[:head, rpart], p.astype(BF16))
-            dk_t[:, cpart] += dot(own_qt[:head, rpart], ds)
-            term = dot(ds, kvbuf[me, 0, cpart])
-            dq = term if dq is None else dq + term
-        dq_acc[rpart] = dq
+    def own_tiles():
+        sums = {}
+        for rb in range(CHUNKS):
+            rpart = pl.ds(rb * qc, qc)
+            aux = own_aux[rpart]
+            q, do = beside(qbuf[me, 0, rpart], aux), beside(qbuf[me, 1, rpart], aux)
+            for cb in range(rb + 1):
+                cpart = pl.ds(cb * kc, kc)
+
+                def first(q=q, do=do, cpart=cpart):
+                    return dot(q, own_kt[:, cpart]), dot(do, own_vt[:, cpart])
+
+                def second(s, d, rb=rb, cb=cb, rpart=rpart, cpart=cpart):
+                    p = jnp.exp2(s * exp_scale)
+                    if cb == rb:
+                        row = lax.broadcasted_iota(jnp.int32, (qc, kc), 0)
+                        col = lax.broadcasted_iota(jnp.int32, (qc, kc), 1)
+                        p = jnp.where(2 * col <= row, p, 0.0)
+                    ds = (p * d).astype(BF16)
+                    dv, dk = dot(own_dot[:head, rpart], p.astype(BF16)), dot(own_qt[:head, rpart], ds)
+                    if cb == rb:
+                        dv_t[:, cpart] = dv
+                        dk_t[:, cpart] = dk
+                    else:
+                        dv_t[:, cpart] += dv
+                        dk_t[:, cpart] += dk
+                    dq = dot(ds, kvbuf[me, 0, cpart])
+                    sums[rb] = sums[rb] + dq if rb in sums else dq
+                    if cb == rb:
+                        dq_acc[rpart] = sums[rb]
+
+                yield first, second
+
+    def run(tiles, lead):
+        waiting = []
+        for first, second in tiles:
+            waiting.append((second, first()))
+            if len(waiting) > lead:
+                second, values = waiting.pop(0)
+                second(*values)
+        for second, values in waiting:
+            second(*values)
+
+    run(own_tiles(), LEAD_D)
 
     def plan(t):
         na, ka = (t - 2) // 2, t % 2
@@ -248,7 +274,7 @@
                 def _():
                     make(src, piece, pair, pair_send.at[idx], recv).start()
 
-    def add_keys_grads(items, cur):
+    def keys_grads(items, cur):
         loaded = []
         for idx, (_, src, piece) in items:
             part = pl.ds(pl.multiple_of(piece * qc, qc), qc)
@@ -256,18 +282,27 @@
             q_t[idx] = jnp.transpose(q)
             do_t[idx] = jnp.transpose(do)
             loaded.append((idx, beside(q, aux), beside(do, aux)))
+        sums = {}
         for cb in range(keys // COLS):
             cpart = pl.ds(cb * COLS, COLS)
-            dv = dk = None
             for idx, q, do in loaded:
-                p = jnp.exp2(dot(q, own_kt[:, cpart]) * exp_scale)
-                ds = (p * dot(do, own_vt[:, cpart])).astype(BF16)
-                tv, tk = dot(do_t[idx], p.astype(BF16)), dot(q_t[idx], ds)
-                dv, dk = (tv, tk) if dv is None else (dv + tv, dk + tk)
-            dv_t[:, cpart] += dv
-            dk_t[:, cpart] += dk
-
-    def add_rows_grad(items):
+                def first(q=q, do=do, cpart=cpart):
+                    return dot(q, own_kt[:, cpart]), dot(do, own_vt[:, cpart])
+
+                def second(s, d, idx=idx, cpart=cpart, cb=cb):
+                    p = jnp.exp2(s * exp_scale)
+                    ds = (p * d).astype(BF16)
+                    dv, dk = dot(do_t[idx], p.astype(BF16)), dot(q_t[idx], ds)
+                    if cb in sums:
+                        dv, dk = sums[cb][0] + dv, sums[cb][1] + dk
+                    sums[cb] = (dv, dk)
+                    if idx == items[-1][0]:
+                        dv_t[:, cpart] += dv
+                        dk_t[:, cpart] += dk
+
+                yield first, second
+
+    def rows_grad(items, width):
         ks, vs = [], []
         for idx, (_, src, piece) in items:
             part = pl.ds(pl.multiple_of(piece * kc, kc), kc)
@@ -277,11 +312,23 @@
         k = jnp.concatenate([beside(k, k_one[...]) for k in ks], axis=0)
         v = jnp.concatenate([beside(v, v_one[...]) for v in vs], axis=0)
         k_t = k_ts[0] if len(k_ts) == 1 else beside(*k_ts)
-        for rb in range(rows // 512):
-            part = pl.ds(rb * 512, 512)
-            p = jnp.exp2(dot(k, own_qt[:, part]) * exp_scale)
-            ds = (p * dot(v, own_dot[:, part])).astype(BF16)
-            dq_t[:, part] += dot(k_t, ds)
+        for rb in range(rows // width):
+            part = pl.ds(rb * width, width)
+
+            def first(part=part):
+                return dot(k, own_qt[:, part]), dot(v, own_dot[:, part])
+
+            def second(s, d, part=part):
+                ds = (jnp.exp2(s * exp_scale) * d).astype(BF16)
+                dq_t[:, part] += dot(k_t, ds)
+
+            yield first, second
+
+    def mixed(xs, ys):
+        xs, ys = list(xs), list(ys)
+        for i in range(max(len(xs), len(ys))):
+            yield from xs[i:i + 1]
+            yield from ys[i:i + 1]
 
     def prefetch(t, idx):
         _, src, piece = plan(t)[idx]
@@ -316,18 +363,17 @@
 
         @pl.when(jnp.logical_not(a_keys))
         def _():
-            add_keys_grads(((0, a), (1, b)), cur)
+            run(keys_grads(((0, a), (1, b)), cur), LEAD_Q)
             ahead()
 
         @pl.when(a_keys & b_keys)
         def _():
-            add_rows_grad(((0, a), (1, b)))
+            run(rows_grad(((0, a), (1, b)), WIDTH_K), LEAD_K)
             ahead()
 
         @pl.when(a_keys & jnp.logical_not(b_keys))
         def _():
-            add_rows_grad(((0, a),))
-            add_keys_grads(((1, b),), cur)
+            run(mixed(rows_grad(((0, a),), WIDTH_M), keys_grads(((1, b),), cur)), LEAD_M)
             ahead()
 
         return 0

time: 53.7 us -> 47.7 us (0.89)
  the two profiles are of different devices: /device:TPU:2 before, /device:TPU:0 now
where the time goes in v5:
time: 47.7 us; the launch traced here: 47.6 us
  Pallas kernels  47 us (99%)
  between operations  0.64 us (1%)
    pallas_call x1, Pallas kernels, local_fn(): pl.pallas_call(functools.partial(kernel, rows, tokens, head, n_dev), out_...  46 us
    pallas_call x1, Pallas kernels, local_fn(): pl.pallas_call(store, out_shape=tuple((jax.ShapeDtypeStruct(g.shape, g.dt...  0.99 us

profile of v5, /device:TPU:0, one launch (start us, length us, event | category | flops | bytes accessed | tf_op | source)
XLA Modules:
  0.0 47.6 jit_solution(2238046801676357399)
XLA Ops:
  0.6 46.0 %attention_backward.1 = (bf16[2048,128]{1,0:T(8,128)(2,1)S(1)}, bf16[1024,128]{1,0:T(8,128)(2,1)S(1)}, bf16[1024,128]{1,0:T(8,128)(2,1)S(1)}) custom-call(bf16[2048,128]{1,0:T(8,128)(2,1)} %bitcast.5, bf16[1024,128]{1,0:T(8,128)(2,1)} %k_hbm.1, bf16[1024,128]{1,0:T(8,128)(2,1)} %v_hbm.1, bf16[2048,128]{1,0:T(8,128)(2,1)} %bitcast.6, ...), custom_call_target="tpu_custom_call" | custom-call | tf_op jit(solution)/shard_map/attention_backward/pallas_call | solution.py:429
  46.6 1.0 %store_grads.1 = (bf16[2048,128]{1,0:T(8,128)(2,1)}, bf16[1024,128]{1,0:T(8,128)(2,1)}, bf16[1024,128]{1,0:T(8,128)(2,1)}) custom-call(bf16[2048,128]{1,0:T(8,128)(2,1)S(1)} %get-tuple-element.9.refs_0_, bf16[1024,128]{1,0:T(8,128)(2,1)S(1)} %get-tuple-element.10.refs_1_, bf16[1024,128]{1,0:T(8,128)(2,1)S(1)} %get-tuple-element.11.refs_2_), custom_call_target="tpu_custom_call" | custom-call | tf_op jit(solution)/shard_map/store_grads/pallas_call | solution.py:471

commit v6 on v5

--- a/solution.py
+++ b/solution.py
@@ -11,7 +11,7 @@
 BF16, F32 = jnp.bfloat16, jnp.float32
 CHUNKS = 4
 COLS = 256
-STEPS = 14
+STEPS, LAST_STEPS = 10, 8
 LEAD_Q, LEAD_K, LEAD_M = 4, 4, 2
 LEAD_D = 2
 WIDTH_K, WIDTH_M = 256, 512
@@ -36,7 +36,7 @@
 def kernel(rows, keys, head, n_dev, q_hbm, k_hbm, v_hbm, o_hbm, do_hbm, lse_hbm, dq_ref, dk_ref, dv_ref,
            qbuf, kvbuf, obuf, lse_in, auxr, own_aux, chunk_aux, k_one, v_one, own_qt, own_dot, own_kt, own_vt,
            q_t, do_t, dq_acc, dq_t, dk_t, dv_t,
-           stage_sem, recv_sem, aux_recv, own_send, own_aux_send, pair_send, x_send, y_send):
+           stage_sem, recv_sem, half_recv, aux_recv, own_send, own_aux_send, pair_send, x_send, y_send):
     me = lax.axis_index('cp')
     core, px, py = me % 2, (me // 2) % 2, me // 4
     pair = me + 1 - 2 * core
@@ -49,14 +49,14 @@
     scale = head ** -0.5
     exp_scale = scale * math.log2(math.e)
 
-    def q_copy(slot, n, dest, send, recv):
-        part = pl.ds(n * qc, qc)
+    def q_copy(slot, n, dest, send, recv, halves=1):
+        part = pl.ds(n * (qc // halves), qc // halves)
         return pltpu.make_async_remote_copy(
             qbuf.at[slot, :, part], qbuf.at[slot, :, part], send, recv,
             device_id={'cp': dest}, device_id_type=MESH)
 
-    def kv_copy(slot, n, dest, send, recv):
-        part = pl.ds(n * kc, kc)
+    def kv_copy(slot, n, dest, send, recv, halves=1):
+        part = pl.ds(n * (kc // halves), kc // halves)
         return pltpu.make_async_remote_copy(
             kvbuf.at[slot, :, part], kvbuf.at[slot, :, part], send, recv,
             device_id={'cp': dest}, device_id_type=MESH)
@@ -132,19 +132,24 @@
 
     def aux_lines(slot, n):
         hi, md, lo = parts(auxr[slot, n])
+        return [stack_lines((hi[g:g + 1], md[g:g + 1], lo[g:g + 1], hi[4 + g:5 + g], md[4 + g:5 + g], lo[4 + g:5 + g]))
+                for g in range(qc // 128)]
+
+    def half_lines(slot, half):
+        n, at = half // 2, (half % 2) * 2
+        return [stack_lines(parts(auxr[slot, n, pl.ds(at + g, 1)]) + parts(auxr[slot, n, pl.ds(4 + at + g, 1)]))
+                for g in range(qc // 256)]
+
+    def stack_lines(lines):
         sub = lax.broadcasted_iota(jnp.int32, (8, 128), 0)
-        lines = []
-        for g in range(qc // 128):
-            m = jnp.zeros((8, 128), F32)
-            for i, row in enumerate((hi[g:g + 1], md[g:g + 1], lo[g:g + 1],
-                                     hi[4 + g:5 + g], md[4 + g:5 + g], lo[4 + g:5 + g])):
-                m = jnp.where(sub == i, row, m)
-            lines.append(jnp.concatenate([m, jnp.zeros((120, 128), F32)], axis=0))
-        return lines
-
-    def fill_aux(slot, n, dst, base):
-        for g, m in enumerate(aux_lines(slot, n)):
-            dst[pl.ds(base + g * 128, 128)] = jnp.transpose(m).astype(BF16)
+        m = jnp.zeros((8, 128), F32)
+        for i, line in enumerate(lines):
+            m = jnp.where(sub == i, line, m)
+        return jnp.concatenate([m, jnp.zeros((120, 128), F32)], axis=0)
+
+    def fill_aux(lines, dst):
+        for g, m in enumerate(lines):
+            dst[pl.ds(g * 128, 128)] = jnp.transpose(m).astype(BF16)
 
     lane = lax.broadcasted_iota(jnp.int32, (COLS, head), 1)
     line = lax.broadcasted_iota(jnp.int32, (head, keys), 0)
@@ -228,19 +233,14 @@
 
     def plan(t):
         na, ka = (t - 2) // 2, t % 2
-        nb = (t - 10) // 2
-        first, second = t < 2, t < 10
+        early = t < 2
         hop = jnp.where(ka == 1, other, 0)
-
-        def pick(a, b, c):
-            return jnp.where(first, a, jnp.where(second, b, c))
-
-        stream_a = pick(3, jnp.where(ka == 0, 0, 3), jnp.where(ka == 0, 2, 3))
-        stream_b = pick(3, jnp.where(ka == 0, 1, 3), jnp.where(ka == 0, 2, 3))
-        src_a = pick(pair, nx + hop, diag + hop)
-        src_b = pick(pair, ny + hop, diag + hop)
-        piece_a = pick(2 * t, (na + 2) % CHUNKS, jnp.where(mid, 2 * nb, nb))
-        piece_b = pick(2 * t + 1, na, jnp.where(mid, 2 * nb + 1, nb + 2))
+        stream_a = jnp.where(early | (ka == 1), 3, 0)
+        stream_b = jnp.where(early | (ka == 1), 3, 1)
+        src_a = jnp.where(early, pair, nx + hop)
+        src_b = jnp.where(early, pair, ny + hop)
+        piece_a = jnp.where(early, 2 * t, (na + 2) % CHUNKS)
+        piece_b = jnp.where(early, 2 * t + 1, na)
         swap = (src_a > me) & (src_b < me)
 
         def swapped(a, b):
@@ -251,9 +251,16 @@
         piece_a, piece_b = swapped(piece_a, piece_b)
         return (stream_a, src_a, piece_a), (stream_b, src_b, piece_b)
 
+    def last_plan(t):
+        n = t // 2
+        src = diag + jnp.where(t % 2 == 1, other, 0)
+        half_a = jnp.where(mid, 2 * n, n)
+        half_b = jnp.where(mid, 2 * n + 1, n + CHUNKS)
+        return src, (half_a, half_b)
+
     def arrive(item):
         stream, src, piece = item
-        idx = jnp.minimum(stream, 2)
+        idx = jnp.minimum(stream, 1)
         recv = recv_sem.at[src, piece]
         to_x = (stream == 1) & (jnp.logical_not(mid) | (piece < 2))
         to_y = (stream == 0) & mid & (piece >= 2)
@@ -264,23 +271,38 @@
 
                 @pl.when(to_x)
                 def _():
-                    make(src, piece, nx, x_send, recv).start()
+                    for h in range(2):
+                        half = 2 * piece + h
+                        make(src, half, nx, x_send, half_recv.at[src, half], 2).start()
 
                 @pl.when(to_y)
                 def _():
-                    make(src, piece, ny, y_send, recv).start()
+                    for h in range(2):
+                        half = 2 * piece + h
+                        make(src, half, ny, y_send, half_recv.at[src, half], 2).start()
 
                 @pl.when(stream < 3)
                 def _():
                     make(src, piece, pair, pair_send.at[idx], recv).start()
 
-    def keys_grads(items, cur):
+    def arrive_half(t, src, half):
+        recv = half_recv.at[src, half]
+        for make, want in ((q_copy, src > me), (kv_copy, src < me)):
+            @pl.when(want)
+            def _():
+                make(src, half, me, x_send, recv, 2).wait_recv()
+
+                @pl.when(t % 2 == 0)
+                def _():
+                    make(src, half, pair, pair_send.at[2], recv, 2).start()
+
+    def keys_grads(items, cur, size):
         loaded = []
-        for idx, (_, src, piece) in items:
-            part = pl.ds(pl.multiple_of(piece * qc, qc), qc)
-            q, do, aux = qbuf[src, 0, part], qbuf[src, 1, part], chunk_aux[cur, idx]
-            q_t[idx] = jnp.transpose(q)
-            do_t[idx] = jnp.transpose(do)
+        for idx, src, piece in items:
+            part = pl.ds(pl.multiple_of(piece * size, size), size)
+            q, do, aux = qbuf[src, 0, part], qbuf[src, 1, part], chunk_aux[cur, idx, :size]
+            q_t[idx, :, :size] = jnp.transpose(q)
+            do_t[idx, :, :size] = jnp.transpose(do)
             loaded.append((idx, beside(q, aux), beside(do, aux)))
         sums = {}
         for cb in range(keys // COLS):
@@ -292,7 +314,7 @@
                 def second(s, d, idx=idx, cpart=cpart, cb=cb):
                     p = jnp.exp2(s * exp_scale)
                     ds = (p * d).astype(BF16)
-                    dv, dk = dot(do_t[idx], p.astype(BF16)), dot(q_t[idx], ds)
+                    dv, dk = dot(do_t[idx, :, :size], p.astype(BF16)), dot(q_t[idx, :, :size], ds)
                     if cb in sums:
                         dv, dk = sums[cb][0] + dv, sums[cb][1] + dk
                     sums[cb] = (dv, dk)
@@ -302,15 +324,15 @@
 
                 yield first, second
 
-    def rows_grad(items, width):
+    def rows_grad(items, width, size):
         ks, vs = [], []
-        for idx, (_, src, piece) in items:
-            part = pl.ds(pl.multiple_of(piece * kc, kc), kc)
+        for idx, src, piece in items:
+            part = pl.ds(pl.multiple_of(piece * size, size), size)
             ks.append(kvbuf[src, 0, part])
             vs.append(kvbuf[src, 1, part])
         k_ts = [jnp.transpose(k) for k in ks]
-        k = jnp.concatenate([beside(k, k_one[...]) for k in ks], axis=0)
-        v = jnp.concatenate([beside(v, v_one[...]) for v in vs], axis=0)
+        k = jnp.concatenate([beside(k, k_one[:size]) for k in ks], axis=0)
+        v = jnp.concatenate([beside(v, v_one[:size]) for v in vs], axis=0)
         k_t = k_ts[0] if len(k_ts) == 1 else beside(*k_ts)
         for rb in range(rows // width):
             part = pl.ds(rb * width, width)
@@ -330,15 +352,22 @@
             yield from xs[i:i + 1]
             yield from ys[i:i + 1]
 
-    def prefetch(t, idx):
-        _, src, piece = plan(t)[idx]
-        fill_aux(jnp.where(src > me, src, me), piece, chunk_aux.at[t % 2, idx], 0)
+    def present(src):
+        return jnp.where(src > me, src, me)
+
+    def ahead(t, slot):
+        for idx, (_, src, piece) in enumerate(plan(t)):
+            fill_aux(aux_lines(present(src), piece), chunk_aux.at[slot, idx])
+
+    def last_ahead(t, slot):
+        src, halves = last_plan(t)
+        for idx, half in enumerate(halves):
+            fill_aux(half_lines(present(src), half), chunk_aux.at[slot, idx])
 
     @pl.when(pair > me)
     def _():
         aux_copy(pair, me, own_aux_send.at[0]).wait_recv()
-        for idx in range(2):
-            prefetch(0, idx)
+        ahead(0, 0)
 
     def step(t, _):
         a, b = plan(t)
@@ -355,34 +384,70 @@
         arrive(b)
         a_keys, b_keys = a[1] < me, b[1] < me
         later = jnp.minimum(t + 1, STEPS - 1)
-
-        def ahead():
-            for idx in range(2):
-                _, src, piece = plan(later)[idx]
-                fill_aux(jnp.where(src > me, src, me), piece, chunk_aux.at[1 - cur, idx], 0)
+        a, b = (0,) + a[1:], (1,) + b[1:]
 
         @pl.when(jnp.logical_not(a_keys))
         def _():
-            run(keys_grads(((0, a), (1, b)), cur), LEAD_Q)
-            ahead()
+            run(keys_grads((a, b), cur, qc), LEAD_Q)
+            ahead(later, 1 - cur)
 
         @pl.when(a_keys & b_keys)
         def _():
-            run(rows_grad(((0, a), (1, b)), WIDTH_K), LEAD_K)
-            ahead()
+            run(rows_grad((a, b), WIDTH_K, kc), LEAD_K)
+            ahead(later, 1 - cur)
 
         @pl.when(a_keys & jnp.logical_not(b_keys))
         def _():
-            run(mixed(rows_grad(((0, a),), WIDTH_M), keys_grads(((1, b),), cur)), LEAD_M)
-            ahead()
+            run(mixed(rows_grad((a,), WIDTH_M, kc), keys_grads((b,), cur, qc)), LEAD_M)
+            ahead(later, 1 - cur)
 
         return 0
 
     lax.fori_loop(0, STEPS, step, 0)
 
-    dq_ref[...] = ((dq_acc[...] + jnp.transpose(dq_t[...])) * scale).astype(BF16)
-    dk_ref[...] = (jnp.transpose(dk_t[...]) * scale).astype(BF16)
-    dv_ref[...] = jnp.transpose(dv_t[...]).astype(BF16)
+    def finish_rows():
+        dq_ref[...] = ((dq_acc[...] + jnp.transpose(dq_t[...])) * scale).astype(BF16)
+
+    def finish_keys():
+        dk_ref[...] = (jnp.transpose(dk_t[...]) * scale).astype(BF16)
+        dv_ref[...] = jnp.transpose(dv_t[...]).astype(BF16)
+
+    @pl.when(diag > me)
+    def _():
+        last_ahead(0, 0)
+        finish_rows()
+
+    @pl.when(diag < me)
+    def _():
+        finish_keys()
+
+    def last_step(t, _):
+        src, halves = last_plan(t)
+        cur = t % 2
+        for half in halves:
+            arrive_half(t, src, half)
+        items = [(idx, src, half) for idx, half in enumerate(halves)]
+
+        @pl.when(src > me)
+        def _():
+            run(keys_grads(items, cur, qc // 2), LEAD_Q)
+            last_ahead(jnp.minimum(t + 1, LAST_STEPS - 1), 1 - cur)
+
+        @pl.when(src < me)
+        def _():
+            run(rows_grad(items, WIDTH_K, kc // 2), LEAD_K)
+
+        return 0
+
+    lax.fori_loop(0, LAST_STEPS, last_step, 0)
+
+    @pl.when(diag > me)
+    def _():
+        finish_keys()
+
+    @pl.when(diag < me)
+    def _():
+        finish_rows()
 
     for peer in range(n_dev):
         @pl.when(peer < me)
@@ -455,6 +520,7 @@
                 vmem((head, tokens), F32),
                 dma((6,)),
                 dma((n_dev, CHUNKS)),
+                dma((n_dev, 2 * CHUNKS)),
                 dma((n_dev,)),
                 dma((3,)),
                 dma((n_dev,)),

time: 47.7 us -> 47.1 us (0.987)
  Pallas kernels: 47 us -> 46.4 us
    pallas_call x1, Pallas kernels: 46 us -> 45.4 us  [local_fn(): pl.pallas_call(functools.partial(kernel, rows, tokens, head, n_dev), out_...]
where the time goes in v6:
time: 47.1 us; the launch traced here: 47 us
  Pallas kernels  46.4 us (99%)
  between operations  0.64 us (1%)
    pallas_call x1, Pallas kernels, local_fn(): pl.pallas_call(functools.partial(kernel, rows, tokens, head, n_dev), out_...  45.4 us
    pallas_call x1, Pallas kernels, local_fn(): pl.pallas_call(store, out_shape=tuple((jax.ShapeDtypeStruct(g.shape, g.dt...  0.99 us

profile of v6, /device:TPU:0, one launch (start us, length us, event | category | flops | bytes accessed | tf_op | source)
XLA Modules:
  0.0 47.0 jit_solution(13940479004236203225)
XLA Ops:
  0.6 45.4 %attention_backward.1 = (bf16[2048,128]{1,0:T(8,128)(2,1)S(1)}, bf16[1024,128]{1,0:T(8,128)(2,1)S(1)}, bf16[1024,128]{1,0:T(8,128)(2,1)S(1)}) custom-call(bf16[2048,128]{1,0:T(8,128)(2,1)} %bitcast.5, bf16[1024,128]{1,0:T(8,128)(2,1)} %k_hbm.1, bf16[1024,128]{1,0:T(8,128)(2,1)} %v_hbm.1, bf16[2048,128]{1,0:T(8,128)(2,1)} %bitcast.6, ...), custom_call_target="tpu_custom_call" | custom-call | tf_op jit(solution)/shard_map/attention_backward/pallas_call | solution.py:494
  46.0 1.0 %store_grads.1 = (bf16[2048,128]{1,0:T(8,128)(2,1)}, bf16[1024,128]{1,0:T(8,128)(2,1)}, bf16[1024,128]{1,0:T(8,128)(2,1)}) custom-call(bf16[2048,128]{1,0:T(8,128)(2,1)S(1)} %get-tuple-element.9.refs_0_, bf16[1024,128]{1,0:T(8,128)(2,1)S(1)} %get-tuple-element.10.refs_1_, bf16[1024,128]{1,0:T(8,128)(2,1)S(1)} %get-tuple-element.11.refs_2_), custom_call_target="tpu_custom_call" | custom-call | tf_op jit(solution)/shard_map/store_grads/pallas_call | solution.py:537

commit v7 on v6

--- a/solution.py
+++ b/solution.py
@@ -90,17 +90,19 @@
     dests = (pair, nx, ny)
     for s in stages[:4]:
         s.wait()
-    for d, dest in enumerate(dests):
-        @pl.when(dest > me)
-        def _():
-            for n in range(CHUNKS):
-                c = order(d, n)
-                kv_copy(me, c, dest, own_send.at[d], recv_sem.at[me, c]).start()
-
-        @pl.when(dest < me)
-        def _():
-            c = order(d, 0)
-            q_copy(me, c, dest, own_send.at[d], recv_sem.at[me, c]).start()
+    def send_keys(d, n):
+        c = order(d, n)
+        kv_copy(me, c, dests[d], own_send.at[d], recv_sem.at[me, c]).start()
+
+    def send_rows(d, n):
+        c = order(d, n)
+        q_copy(me, c, dests[d], own_send.at[d], recv_sem.at[me, c]).start()
+
+    for n in range(CHUNKS):
+        for d in (1, 2, 0):
+            pl.when(dests[d] > me)(functools.partial(send_keys, d, n))
+            if n == 0:
+                pl.when(dests[d] < me)(functools.partial(send_rows, d, n))
 
     for s in stages[4:]:
         s.wait()
@@ -179,12 +181,9 @@
         @pl.when(peer < me)
         def _():
             aux_copy(me, peer, own_aux_send.at[peer]).start()
-    for d, dest in enumerate(dests):
-        @pl.when(dest < me)
-        def _():
-            for n in range(1, CHUNKS):
-                c = order(d, n)
-                q_copy(me, c, dest, own_send.at[d], recv_sem.at[me, c]).start()
+    for n in range(1, CHUNKS):
+        for d in (1, 2, 0):
+            pl.when(dests[d] < me)(functools.partial(send_rows, d, n))
 
     def own_tiles():
         sums = {}

time: 47.1 us -> 47.1 us (level)
  no operation moved by 1% of the time
where the time goes in v7:
time: 47.1 us; the launch traced here: 47 us
  Pallas kernels  46.4 us (99%)
  between operations  0.64 us (1%)
    pallas_call x1, Pallas kernels, local_fn(): pl.pallas_call(functools.partial(kernel, rows, tokens, head, n_dev), out_...  45.4 us
    pallas_call x1, Pallas kernels, local_fn(): pl.pallas_call(store, out_shape=tuple((jax.ShapeDtypeStruct(g.shape, g.dt...  0.99 us

profile of v7, /device:TPU:0, one launch (start us, length us, event | category | flops | bytes accessed | tf_op | source)
XLA Modules:
  0.0 47.0 jit_solution(11885222401194029400)
XLA Ops:
  0.6 45.4 %attention_backward.1 = (bf16[2048,128]{1,0:T(8,128)(2,1)S(1)}, bf16[1024,128]{1,0:T(8,128)(2,1)S(1)}, bf16[1024,128]{1,0:T(8,128)(2,1)S(1)}) custom-call(bf16[2048,128]{1,0:T(8,128)(2,1)} %bitcast.5, bf16[1024,128]{1,0:T(8,128)(2,1)} %k_hbm.1, bf16[1024,128]{1,0:T(8,128)(2,1)} %v_hbm.1, bf16[2048,128]{1,0:T(8,128)(2,1)} %bitcast.6, ...), custom_call_target="tpu_custom_call" | custom-call | tf_op jit(solution)/shard_map/attention_backward/pallas_call | solution.py:493
  46.0 1.0 %store_grads.1 = (bf16[2048,128]{1,0:T(8,128)(2,1)}, bf16[1024,128]{1,0:T(8,128)(2,1)}, bf16[1024,128]{1,0:T(8,128)(2,1)}) custom-call(bf16[2048,128]{1,0:T(8,128)(2,1)S(1)} %get-tuple-element.9.refs_0_, bf16[1024,128]{1,0:T(8,128)(2,1)S(1)} %get-tuple-element.10.refs_1_, bf16[1024,128]{1,0:T(8,128)(2,1)S(1)} %get-tuple-element.11.refs_2_), custom_call_target="tpu_custom_call" | custom-call | tf_op jit(solution)/shard_map/store_grads/pallas_call | solution.py:536

commit v8 on v7

--- a/solution.py
+++ b/solution.py
@@ -36,7 +36,7 @@
 def kernel(rows, keys, head, n_dev, q_hbm, k_hbm, v_hbm, o_hbm, do_hbm, lse_hbm, dq_ref, dk_ref, dv_ref,
            qbuf, kvbuf, obuf, lse_in, auxr, own_aux, chunk_aux, k_one, v_one, own_qt, own_dot, own_kt, own_vt,
            q_t, do_t, dq_acc, dq_t, dk_t, dv_t,
-           stage_sem, recv_sem, half_recv, aux_recv, own_send, own_aux_send, pair_send, x_send, y_send):
+           stage_sem, recv_sem, half_recv, aux_recv, own_send, own_aux_send, pair_send, pair_aux_send, x_send, y_send, x_aux_send):
     me = lax.axis_index('cp')
     core, px, py = me % 2, (me // 2) % 2, me // 4
     pair = me + 1 - 2 * core
@@ -67,10 +67,10 @@
             device_id={'cp': dest}, device_id_type=MESH)
 
     stages = [
-        pltpu.make_async_copy(k_hbm, kvbuf.at[me, 0], stage_sem.at[0]),
-        pltpu.make_async_copy(v_hbm, kvbuf.at[me, 1], stage_sem.at[1]),
-        pltpu.make_async_copy(q_hbm, qbuf.at[me, 0], stage_sem.at[2]),
-        pltpu.make_async_copy(do_hbm, qbuf.at[me, 1], stage_sem.at[3]),
+        pltpu.make_async_copy(q_hbm, qbuf.at[me, 0], stage_sem.at[0]),
+        pltpu.make_async_copy(do_hbm, qbuf.at[me, 1], stage_sem.at[1]),
+        pltpu.make_async_copy(k_hbm, kvbuf.at[me, 0], stage_sem.at[2]),
+        pltpu.make_async_copy(v_hbm, kvbuf.at[me, 1], stage_sem.at[3]),
         pltpu.make_async_copy(o_hbm, obuf, stage_sem.at[4]),
         pltpu.make_async_copy(lse_hbm, lse_in, stage_sem.at[5]),
     ]
@@ -78,17 +78,15 @@
         s.start()
 
     barrier = pltpu.get_barrier_semaphore()
-    for peer in range(n_dev):
-        @pl.when(peer != me)
-        def _():
-            pl.semaphore_signal(barrier, inc=1, device_id={'cp': peer}, device_id_type=MESH)
-    pl.semaphore_wait(barrier, n_dev - 1)
+    for peer in (nx, ny, pair):
+        pl.semaphore_signal(barrier, inc=1, device_id={'cp': peer}, device_id_type=MESH)
+    pl.semaphore_wait(barrier, 3)
 
     def order(d, n):
         return (n + 2) % CHUNKS if d == 1 else n
 
     dests = (pair, nx, ny)
-    for s in stages[:4]:
+    for s in stages[:2]:
         s.wait()
     def send_keys(d, n):
         c = order(d, n)
@@ -98,11 +96,14 @@
         c = order(d, n)
         q_copy(me, c, dests[d], own_send.at[d], recv_sem.at[me, c]).start()
 
+    for d in (1, 2):
+        pl.when(dests[d] < me)(functools.partial(send_rows, d, 0))
+    for s in stages[2:4]:
+        s.wait()
     for n in range(CHUNKS):
         for d in (1, 2, 0):
             pl.when(dests[d] > me)(functools.partial(send_keys, d, n))
-            if n == 0:
-                pl.when(dests[d] < me)(functools.partial(send_rows, d, n))
+    pl.when(pair < me)(functools.partial(send_rows, 0, 0))
 
     for s in stages[4:]:
         s.wait()
@@ -177,10 +178,10 @@
 
     lax.fori_loop(0, CHUNKS, own_fill, 0)
 
-    for peer in range(n_dev):
-        @pl.when(peer < me)
-        def _():
-            aux_copy(me, peer, own_aux_send.at[peer]).start()
+    for d, dest in enumerate(dests):
+        @pl.when(dest < me)
+        def _():
+            aux_copy(me, dest, own_aux_send.at[d]).start()
     for n in range(1, CHUNKS):
         for d in (1, 2, 0):
             pl.when(dests[d] < me)(functools.partial(send_rows, d, n))
@@ -363,9 +364,17 @@
         for idx, half in enumerate(halves):
             fill_aux(half_lines(present(src), half), chunk_aux.at[slot, idx])
 
+    def take_lines(src, to_pair=None):
+        @pl.when(src > me)
+        def _():
+            aux_copy(src, me, x_aux_send).wait_recv()
+            if to_pair is not None:
+                aux_copy(src, pair, pair_aux_send.at[to_pair]).start()
+
+    take_lines(pair)
+
     @pl.when(pair > me)
     def _():
-        aux_copy(pair, me, own_aux_send.at[0]).wait_recv()
         ahead(0, 0)
 
     def step(t, _):
@@ -374,10 +383,17 @@
 
         @pl.when(t == 1)
         def _():
-            for peer in range(n_dev):
-                @pl.when((peer > me) & (peer != pair))
-                def _():
-                    aux_copy(peer, me, own_aux_send.at[0]).wait_recv()
+            take_lines(nx, 0)
+            take_lines(ny, 1)
+
+            @pl.when(ny > me)
+            def _():
+                aux_copy(ny, nx, x_aux_send).start()
+
+        @pl.when(t == 2)
+        def _():
+            take_lines(nx + other)
+            take_lines(ny + other)
 
         arrive(a)
         arrive(b)
@@ -411,6 +427,32 @@
         dk_ref[...] = (jnp.transpose(dk_t[...]) * scale).astype(BF16)
         dv_ref[...] = jnp.transpose(dv_t[...]).astype(BF16)
 
+    take_lines(diag, 2)
+    def left(buf, slot, length, send, want):
+        @pl.when(want)
+        def _():
+            block = buf.at[slot, :, pl.ds(0, length)]
+            pltpu.make_async_remote_copy(block, block, send, recv_sem.at[slot, 0],
+                                         device_id={'cp': pair}, device_id_type=MESH).wait_send()
+
+    sides = ((qbuf, rows, 1), (kvbuf, keys, -1))
+    for buf, size, sign in sides:
+        for d, dest in enumerate(dests):
+            left(buf, me, size, own_send.at[d], sign * dest < sign * me)
+        for d, src in enumerate((nx, ny)):
+            left(buf, src, size, pair_send.at[d], sign * src > sign * me)
+    for d, dest in enumerate(dests):
+        @pl.when(dest < me)
+        def _():
+            aux_copy(me, dest, own_aux_send.at[d]).wait_send()
+    for d, src in enumerate((nx, ny)):
+        @pl.when(src > me)
+        def _():
+            aux_copy(src, pair, pair_aux_send.at[d]).wait_send()
+
+            if d == 1:
+                aux_copy(src, nx, x_aux_send).wait_send()
+
     @pl.when(diag > me)
     def _():
         last_ahead(0, 0)
@@ -419,6 +461,8 @@
     @pl.when(diag < me)
     def _():
         finish_keys()
+
+    take_lines(diag + other)
 
     def last_step(t, _):
         src, halves = last_plan(t)
@@ -448,26 +492,15 @@
     def _():
         finish_rows()
 
-    for peer in range(n_dev):
-        @pl.when(peer < me)
-        def _():
-            aux_copy(me, peer, own_aux_send.at[peer]).wait_send()
-
-    def left(buf, slot, length, send, want):
-        @pl.when(want)
-        def _():
-            block = buf.at[slot, :, pl.ds(0, length)]
-            pltpu.make_async_remote_copy(block, block, send, recv_sem.at[slot, 0],
-                                         device_id={'cp': pair}, device_id_type=MESH).wait_send()
-
-    for buf, size, sign in ((qbuf, rows, 1), (kvbuf, keys, -1)):
-        for d, dest in enumerate(dests):
-            left(buf, me, size, own_send.at[d], sign * dest < sign * me)
-        for d, src in enumerate((nx, ny, diag)):
-            left(buf, src, size, pair_send.at[d], sign * src > sign * me)
+    for buf, size, sign in sides:
+        left(buf, diag, size, pair_send.at[2], sign * diag > sign * me)
         left(buf, ny, size, x_send, (sign * ny > sign * me) & jnp.logical_not(mid))
         left(buf, ny, size // 2, x_send, (sign * ny > sign * me) & mid)
         left(buf, nx, size // 2, y_send, (sign * nx > sign * me) & mid)
+
+    @pl.when(diag > me)
+    def _():
+        aux_copy(diag, pair, pair_aux_send.at[2]).wait_send()
 
 
 def store(*refs):
@@ -522,8 +555,10 @@
                 dma((n_dev, 2 * CHUNKS)),
                 dma((n_dev,)),
                 dma((3,)),
-                dma((n_dev,)),
                 dma((3,)),
+                dma((3,)),
+                dma((3,)),
+                dma,
                 dma,
                 dma,
             ],

time: 47.1 us -> 46.3 us (0.983)
  Pallas kernels: 46.4 us -> 45.6 us
    pallas_call x1, Pallas kernels: 45.4 us -> 44.6 us  [local_fn(): pl.pallas_call(functools.partial(kernel, rows, tokens, head, n_dev), out_...]
where the time goes in v8:
time: 46.3 us; the launch traced here: 46.2 us
  Pallas kernels  45.6 us (98%)
  between operations  0.64 us (1%)
    pallas_call x1, Pallas kernels, local_fn(): pl.pallas_call(functools.partial(kernel, rows, tokens, head, n_dev), out_...  44.6 us
    pallas_call x1, Pallas kernels, local_fn(): pl.pallas_call(store, out_shape=tuple((jax.ShapeDtypeStruct(g.shape, g.dt...  0.99 us

profile of v8, /device:TPU:0, one launch (start us, length us, event | category | flops | bytes accessed | tf_op | source)
XLA Modules:
  0.0 46.2 jit_solution(5562500380996473443)
XLA Ops:
  0.6 44.6 %attention_backward.1 = (bf16[2048,128]{1,0:T(8,128)(2,1)S(1)}, bf16[1024,128]{1,0:T(8,128)(2,1)S(1)}, bf16[1024,128]{1,0:T(8,128)(2,1)S(1)}) custom-call(bf16[2048,128]{1,0:T(8,128)(2,1)} %bitcast.5, bf16[1024,128]{1,0:T(8,128)(2,1)} %k_hbm.1, bf16[1024,128]{1,0:T(8,128)(2,1)} %v_hbm.1, bf16[2048,128]{1,0:T(8,128)(2,1)} %bitcast.6, ...), custom_call_target="tpu_custom_call" | custom-call | tf_op jit(solution)/shard_map/attention_backward/pallas_call | solution.py:526
  45.2 1.0 %store_grads.1 = (bf16[2048,128]{1,0:T(8,128)(2,1)}, bf16[1024,128]{1,0:T(8,128)(2,1)}, bf16[1024,128]{1,0:T(8,128)(2,1)}) custom-call(bf16[2048,128]{1,0:T(8,128)(2,1)S(1)} %get-tuple-element.9.refs_0_, bf16[1024,128]{1,0:T(8,128)(2,1)S(1)} %get-tuple-element.10.refs_1_, bf16[1024,128]{1,0:T(8,128)(2,1)S(1)} %get-tuple-element.11.refs_2_), custom_call_target="tpu_custom_call" | custom-call | tf_op jit(solution)/shard_map/store_grads/pallas_call | solution.py:571

commit v9 on v8

--- a/solution.py
+++ b/solution.py
@@ -12,8 +12,9 @@
 CHUNKS = 4
 COLS = 256
 STEPS, LAST_STEPS = 10, 8
-LEAD_Q, LEAD_K, LEAD_M = 4, 4, 2
+LEAD_Q, LEAD_K, LEAD_M = 2, 4, 2
 LEAD_D = 2
+ROWS_Q = 256
 WIDTH_K, WIDTH_M = 256, 512
 MESH = pl.DeviceIdType.MESH
 
@@ -108,31 +109,6 @@
     for s in stages[4:]:
         s.wait()
 
-    at_row = lax.broadcasted_iota(jnp.int32, (COLS, COLS), 0)
-    at_col = lax.broadcasted_iota(jnp.int32, (COLS, COLS), 1)
-    weave = jnp.where(at_col == 2 * (at_row % 128) + at_row // 128, 1.0, 0.0).astype(BF16)
-    sub = lax.broadcasted_iota(jnp.int32, (16, 128), 0)
-    for g in range(rows // 256):
-        sides = []
-        for h in range(2):
-            row = lse_in[h:h + 1, g * 128:(g + 1) * 128] * (1.0 / scale)
-            hi, md, lo = parts(row)
-            sides.append(jnp.where(sub == 0, hi, jnp.where(sub == 1, md, jnp.where(sub == 2, lo, 0.0))))
-        woven = dot(beside(*sides).astype(BF16), weave)
-        row = woven[0:1] + (woven[1:2] + woven[2:3])
-        n, at = g // 2, (g % 2) * 2
-        auxr[me, n, at:at + 1] = row[:, 0:128]
-        auxr[me, n, at + 1:at + 2] = row[:, 128:256]
-
-    def delta_rows(n, _):
-        for g in range(qc // 128):
-            part = pl.ds(pl.multiple_of(n * qc + g * 128, 128), 128)
-            d = jnp.sum(qbuf[me, 1, part].astype(F32) * obuf[part].astype(F32), axis=1, keepdims=True)
-            auxr[me, n, 4 + g:5 + g] = jnp.transpose(jnp.broadcast_to(d, (128, 128)))[0:1]
-        return 0
-
-    lax.fori_loop(0, CHUNKS, delta_rows, 0)
-
     def aux_lines(slot, n):
         hi, md, lo = parts(auxr[slot, n])
         return [stack_lines((hi[g:g + 1], md[g:g + 1], lo[g:g + 1], hi[4 + g:5 + g], md[4 + g:5 + g], lo[4 + g:5 + g]))
@@ -148,11 +124,37 @@
         m = jnp.zeros((8, 128), F32)
         for i, line in enumerate(lines):
             m = jnp.where(sub == i, line, m)
-        return jnp.concatenate([m, jnp.zeros((120, 128), F32)], axis=0)
+        return m
 
     def fill_aux(lines, dst):
         for g, m in enumerate(lines):
+            m = jnp.concatenate([m, jnp.zeros((120, 128), F32)], axis=0)
             dst[pl.ds(g * 128, 128)] = jnp.transpose(m).astype(BF16)
+
+    at_row = lax.broadcasted_iota(jnp.int32, (COLS, COLS), 0)
+    at_col = lax.broadcasted_iota(jnp.int32, (COLS, COLS), 1)
+    weave = jnp.where(at_col == 2 * (at_row % 128) + at_row // 128, 1.0, 0.0).astype(BF16)
+    sub = lax.broadcasted_iota(jnp.int32, (16, 128), 0)
+    for n in range(CHUNKS):
+        part = pl.ds(n * qc, qc)
+        do_turned = jnp.transpose(qbuf[me, 1, part])
+        own_dot[:head, part] = do_turned
+        sums = jnp.sum(do_turned.astype(F32) * jnp.transpose(obuf[part]).astype(F32), axis=0, keepdims=True)
+        for g in range(qc // 128):
+            auxr[me, n, 4 + g:5 + g] = sums[:, g * 128:(g + 1) * 128]
+        for g in range(qc // 256):
+            sides = []
+            for h in range(2):
+                at = n * (qc // 2) + g * 128
+                hi, md, lo = parts(lse_in[h:h + 1, at:at + 128] * (1.0 / scale))
+                sides.append(jnp.where(sub == 0, hi, jnp.where(sub == 1, md, jnp.where(sub == 2, lo, 0.0))))
+            woven = dot(beside(*sides).astype(BF16), weave)
+            row = woven[0:1] + (woven[1:2] + woven[2:3])
+            auxr[me, n, 2 * g:2 * g + 1] = row[:, 0:128]
+            auxr[me, n, 2 * g + 1:2 * g + 2] = row[:, 128:256]
+
+    for n in range(1, CHUNKS):
+        pl.when(pair < me)(functools.partial(send_rows, 0, n))
 
     lane = lax.broadcasted_iota(jnp.int32, (COLS, head), 1)
     line = lax.broadcasted_iota(jnp.int32, (head, keys), 0)
@@ -161,29 +163,24 @@
     own_kt[head:] = jnp.where(line < 3, -1.0, 0.0).astype(BF16)
     own_vt[head:] = jnp.where((line >= 3) & (line < 6), -1.0, 0.0).astype(BF16)
     dq_t[...] = jnp.zeros_like(dq_t)
-
-    def own_fill(n, _):
-        base = pl.multiple_of(n * qc, 128)
-        part, kpart = pl.ds(base, qc), pl.ds(pl.multiple_of(n * kc, 128), kc)
-        for g, m in enumerate(aux_lines(me, n)):
-            at = pl.ds(pl.multiple_of(base + g * 128, 128), 128)
-            own_aux[at] = jnp.transpose(m).astype(BF16)
-            own_qt[head:, at] = m.astype(BF16)
-            own_dot[head:, at] = m.astype(BF16)
+    for n in range(CHUNKS):
+        part, kpart = pl.ds(n * qc, qc), pl.ds(n * kc, kc)
+        lines = aux_lines(me, n)
+        fill_aux(lines, own_aux.at[part])
+        for g, m in enumerate(lines):
+            m = jnp.concatenate([m, jnp.zeros((120, 128), F32)], axis=0).astype(BF16)
+            own_qt[head:, pl.ds(n * qc + g * 128, 128)] = m
+            own_dot[head:, pl.ds(n * qc + g * 128, 128)] = m
         own_qt[:head, part] = jnp.transpose(qbuf[me, 0, part])
-        own_dot[:head, part] = jnp.transpose(qbuf[me, 1, part])
         own_kt[:head, kpart] = jnp.transpose(kvbuf[me, 0, kpart])
         own_vt[:head, kpart] = jnp.transpose(kvbuf[me, 1, kpart])
-        return 0
-
-    lax.fori_loop(0, CHUNKS, own_fill, 0)
 
     for d, dest in enumerate(dests):
         @pl.when(dest < me)
         def _():
             aux_copy(me, dest, own_aux_send.at[d]).start()
     for n in range(1, CHUNKS):
-        for d in (1, 2, 0):
+        for d in (1, 2):
             pl.when(dests[d] < me)(functools.partial(send_rows, d, n))
 
     def own_tiles():
@@ -305,24 +302,28 @@
             do_t[idx, :, :size] = jnp.transpose(do)
             loaded.append((idx, beside(q, aux), beside(do, aux)))
         sums = {}
+        last = (items[-1][0], size - min(size, ROWS_Q))
         for cb in range(keys // COLS):
             cpart = pl.ds(cb * COLS, COLS)
             for idx, q, do in loaded:
-                def first(q=q, do=do, cpart=cpart):
-                    return dot(q, own_kt[:, cpart]), dot(do, own_vt[:, cpart])
-
-                def second(s, d, idx=idx, cpart=cpart, cb=cb):
-                    p = jnp.exp2(s * exp_scale)
-                    ds = (p * d).astype(BF16)
-                    dv, dk = dot(do_t[idx, :, :size], p.astype(BF16)), dot(q_t[idx, :, :size], ds)
-                    if cb in sums:
-                        dv, dk = sums[cb][0] + dv, sums[cb][1] + dk
-                    sums[cb] = (dv, dk)
-                    if idx == items[-1][0]:
-                        dv_t[:, cpart] += dv
-                        dk_t[:, cpart] += dk
-
-                yield first, second
+                for at in range(0, size, ROWS_Q):
+                    part = slice(at, min(size, at + ROWS_Q))
+
+                    def first(q=q, do=do, part=part, cpart=cpart):
+                        return dot(q[part], own_kt[:, cpart]), dot(do[part], own_vt[:, cpart])
+
+                    def second(s, d, idx=idx, part=part, cpart=cpart, cb=cb):
+                        p = jnp.exp2(s * exp_scale)
+                        ds = (p * d).astype(BF16)
+                        dv, dk = dot(do_t[idx, :, part], p.astype(BF16)), dot(q_t[idx, :, part], ds)
+                        if cb in sums:
+                            dv, dk = sums[cb][0] + dv, sums[cb][1] + dk
+                        sums[cb] = (dv, dk)
+                        if (idx, part.start) == last:
+                            dv_t[:, cpart] += dv
+                            dk_t[:, cpart] += dk
+
+                    yield first, second
 
     def rows_grad(items, width, size):
         ks, vs = [], []

time: 46.3 us -> 46.7 us (level)
  no operation moved by 1% of the time
where the time goes in v9:
time: 46.7 us; the launch traced here: 46.6 us
  Pallas kernels  46 us (99%)
  between operations  0.64 us (1%)
    pallas_call x1, Pallas kernels, local_fn(): pl.pallas_call(functools.partial(kernel, rows, tokens, head, n_dev), out_...  45 us
    pallas_call x1, Pallas kernels, local_fn(): pl.pallas_call(store, out_shape=tuple((jax.ShapeDtypeStruct(g.shape, g.dt...  0.99 us

profile of v9, /device:TPU:0, one launch (start us, length us, event | category | flops | bytes accessed | tf_op | source)
XLA Modules:
  0.0 46.6 jit_solution(16751076772304040943)
XLA Ops:
  0.6 45.0 %attention_backward.1 = (bf16[2048,128]{1,0:T(8,128)(2,1)S(1)}, bf16[1024,128]{1,0:T(8,128)(2,1)S(1)}, bf16[1024,128]{1,0:T(8,128)(2,1)S(1)}) custom-call(bf16[2048,128]{1,0:T(8,128)(2,1)} %bitcast.5, bf16[1024,128]{1,0:T(8,128)(2,1)} %k_hbm.1, bf16[1024,128]{1,0:T(8,128)(2,1)} %v_hbm.1, bf16[2048,128]{1,0:T(8,128)(2,1)} %bitcast.6, ...), custom_call_target="tpu_custom_call" | custom-call | tf_op jit(solution)/shard_map/attention_backward/pallas_call | solution.py:527
  45.6 1.0 %store_grads.1 = (bf16[2048,128]{1,0:T(8,128)(2,1)}, bf16[1024,128]{1,0:T(8,128)(2,1)}, bf16[1024,128]{1,0:T(8,128)(2,1)}) custom-call(bf16[2048,128]{1,0:T(8,128)(2,1)S(1)} %get-tuple-element.9.refs_0_, bf16[1024,128]{1,0:T(8,128)(2,1)S(1)} %get-tuple-element.10.refs_1_, bf16[1024,128]{1,0:T(8,128)(2,1)S(1)} %get-tuple-element.11.refs_2_), custom_call_target="tpu_custom_call" | custom-call | tf_op jit(solution)/shard_map/store_grads/pallas_call | solution.py:572

commit v10 on v9

--- a/solution.py
+++ b/solution.py
@@ -12,9 +12,10 @@
 CHUNKS = 4
 COLS = 256
 STEPS, LAST_STEPS = 10, 8
-LEAD_Q, LEAD_K, LEAD_M = 2, 4, 2
+LEAD_Q, LEAD_K, LEAD_M = 4, 4, 2
 LEAD_D = 2
-ROWS_Q = 256
+LEAD_LQ, LEAD_LK, WIDTH_L = 6, 3, 512
+ROWS_Q = 512
 WIDTH_K, WIDTH_M = 256, 512
 MESH = pl.DeviceIdType.MESH
 
@@ -270,20 +271,20 @@
                 def _():
                     for h in range(2):
                         half = 2 * piece + h
-                        make(src, half, nx, x_send, half_recv.at[src, half], 2).start()
+                        make(src, half, nx, x_send, half_recv.at[src % 2, half], 2).start()
 
                 @pl.when(to_y)
                 def _():
                     for h in range(2):
                         half = 2 * piece + h
-                        make(src, half, ny, y_send, half_recv.at[src, half], 2).start()
+                        make(src, half, ny, y_send, half_recv.at[src % 2, half], 2).start()
 
                 @pl.when(stream < 3)
                 def _():
                     make(src, piece, pair, pair_send.at[idx], recv).start()
 
     def arrive_half(t, src, half):
-        recv = half_recv.at[src, half]
+        recv = half_recv.at[src % 2, half]
         for make, want in ((q_copy, src > me), (kv_copy, src < me)):
             @pl.when(want)
             def _():
@@ -474,12 +475,12 @@
 
         @pl.when(src > me)
         def _():
-            run(keys_grads(items, cur, qc // 2), LEAD_Q)
+            run(keys_grads(items, cur, qc // 2), LEAD_LQ)
             last_ahead(jnp.minimum(t + 1, LAST_STEPS - 1), 1 - cur)
 
         @pl.when(src < me)
         def _():
-            run(rows_grad(items, WIDTH_K, kc // 2), LEAD_K)
+            run(rows_grad(items, WIDTH_L, kc // 2), LEAD_LK)
 
         return 0
 
@@ -553,7 +554,7 @@
                 vmem((head, tokens), F32),
                 dma((6,)),
                 dma((n_dev, CHUNKS)),
-                dma((n_dev, 2 * CHUNKS)),
+                dma((2, 2 * CHUNKS)),
                 dma((n_dev,)),
                 dma((3,)),
                 dma((3,)),

time: 46.7 us -> 45.9 us (0.983)
  Pallas kernels: 46 us -> 45.2 us
    pallas_call x1, Pallas kernels: 45 us -> 44.2 us  [local_fn(): pl.pallas_call(functools.partial(kernel, rows, tokens, head, n_dev), out_...]
where the time goes in v10:
time: 45.9 us; the launch traced here: 45.8 us
  Pallas kernels  45.2 us (98%)
  between operations  0.64 us (1%)
    pallas_call x1, Pallas kernels, local_fn(): pl.pallas_call(functools.partial(kernel, rows, tokens, head, n_dev), out_...  44.2 us
    pallas_call x1, Pallas kernels, local_fn(): pl.pallas_call(store, out_shape=tuple((jax.ShapeDtypeStruct(g.shape, g.dt...  0.99 us

profile of v10, /device:TPU:0, one launch (start us, length us, event | category | flops | bytes accessed | tf_op | source)
XLA Modules:
  0.0 45.8 jit_solution(2359492058266520492)
XLA Ops:
  0.6 44.2 %attention_backward.1 = (bf16[2048,128]{1,0:T(8,128)(2,1)S(1)}, bf16[1024,128]{1,0:T(8,128)(2,1)S(1)}, bf16[1024,128]{1,0:T(8,128)(2,1)S(1)}) custom-call(bf16[2048,128]{1,0:T(8,128)(2,1)} %bitcast.5, bf16[1024,128]{1,0:T(8,128)(2,1)} %k_hbm.1, bf16[1024,128]{1,0:T(8,128)(2,1)} %v_hbm.1, bf16[2048,128]{1,0:T(8,128)(2,1)} %bitcast.6, ...), custom_call_target="tpu_custom_call" | custom-call | tf_op jit(solution)/shard_map/attention_backward/pallas_call | solution.py:528
  44.8 1.0 %store_grads.1 = (bf16[2048,128]{1,0:T(8,128)(2,1)}, bf16[1024,128]{1,0:T(8,128)(2,1)}, bf16[1024,128]{1,0:T(8,128)(2,1)}) custom-call(bf16[2048,128]{1,0:T(8,128)(2,1)S(1)} %get-tuple-element.9.refs_0_, bf16[1024,128]{1,0:T(8,128)(2,1)S(1)} %get-tuple-element.10.refs_1_, bf16[1024,128]{1,0:T(8,128)(2,1)S(1)} %get-tuple-element.11.refs_2_), custom_call_target="tpu_custom_call" | custom-call | tf_op jit(solution)/shard_map/store_grads/pallas_call | solution.py:573
